TPU v7x, 32 devices: a whole 2x2x4 slice. The times are simulated.
32 devices in a mesh: data: 32 (over z, y, x, core).
Axes of the slice: x: 2, y: 2, z: 4, core: 2. Of those that a mesh axis runs over, the one named last changes fastest.
Arguments:
- tokens: bfloat16 [65536, 768], P('data')
- upstream: bfloat16 [65536, 768], P('data')
- norm_gain: bfloat16 [2, 768], replicated
- w_up: bfloat16 [2, 768, 3072], replicated
- bias_up: bfloat16 [2, 3072], replicated
- w_down: bfloat16 [2, 3072, 768], replicated
- bias_down: bfloat16 [2, 768], replicated
Outputs:
- output 1: float32 [2, 768], replicated
- output 2: float32 [2, 768, 3072], replicated
- output 3: float32 [2, 3072], replicated
- output 4: float32 [2, 3072, 768], replicated
- output 5: float32 [2, 768], replicated
All inputs are finite; a program needn't handle non-finite values.
Results may differ from a plain program's by a relative error of at most 0.00727116.
Values are sent between devices in bfloat16 or wider.
A program may use at most 1 GiB of HBM per device.

v0:
```python
import jax
import jax.numpy as jnp
from jax import lax
from jax.sharding import PartitionSpec as P

EPSILON = 1e-6
TOKEN_DIMS = (((0,), (0,)), ((), ()))
FEATURE_DIMS = (((1,), (1,)), ((), ()))


def gelu_tanh(values):
    return jax.nn.gelu(values, approximate=True)


def inverse_rms(hid_f):
    return lax.rsqrt(jnp.mean(hid_f * hid_f, axis=-1, keepdims=True) + EPSILON)


def forward_stack(hidden, norm_gain, w_up, bias_up, w_down, bias_down):
    saved_acts = []
    for layer_idx in range(norm_gain.shape[0]):
        hid_f = hidden.astype(jnp.float32)
        hid_scale = inverse_rms(hid_f)
        hid_hat = hid_f * hid_scale
        normed = (hid_hat * norm_gain[layer_idx].astype(jnp.float32)).astype(jnp.bfloat16)
        pre_act = (jnp.dot(normed, w_up[layer_idx], preferred_element_type=jnp.float32) + bias_up[layer_idx].astype(jnp.float32)).astype(jnp.bfloat16)
        activated = gelu_tanh(pre_act.astype(jnp.float32)).astype(jnp.bfloat16)
        branch = jnp.dot(activated, w_down[layer_idx], preferred_element_type=jnp.float32)
        hidden = (hid_f + branch + bias_down[layer_idx].astype(jnp.float32)).astype(jnp.bfloat16)
        saved_acts.append((hid_scale, hid_hat, normed, pre_act, activated))
    return hidden, saved_acts


def top_gradient(top_hidden, upstream):
    top_f = top_hidden.astype(jnp.float32)
    top_scale = inverse_rms(top_f)
    top_hat = top_f * top_scale
    up_f = upstream.astype(jnp.float32)
    return top_scale * (up_f - top_hat * jnp.mean(up_f * top_hat, axis=-1, keepdims=True))


def layer_backward(grad_h, saved_layer, gain_row, up_mat, down_mat, need_input):
    hid_scale, hid_hat, normed, pre_act, activated = saved_layer
    grad_b = grad_h.astype(jnp.bfloat16)
    grad_down = lax.dot_general(activated, grad_b, TOKEN_DIMS, preferred_element_type=jnp.float32)
    grad_down_bias = jnp.sum(grad_h, axis=0)
    grad_act = lax.dot_general(grad_b, down_mat, FEATURE_DIMS, preferred_element_type=jnp.float32)
    gelu_back = jax.vjp(gelu_tanh, pre_act.astype(jnp.float32))[1]
    grad_pre = gelu_back(grad_act)[0]
    grad_pre_b = grad_pre.astype(jnp.bfloat16)
    grad_up = lax.dot_general(normed, grad_pre_b, TOKEN_DIMS, preferred_element_type=jnp.float32)
    grad_up_bias = jnp.sum(grad_pre, axis=0)
    grad_normed = lax.dot_general(grad_pre_b, up_mat, FEATURE_DIMS, preferred_element_type=jnp.float32)
    grad_gain = jnp.sum(grad_normed * hid_hat, axis=0)
    layer_grads = (grad_gain, grad_up, grad_up_bias, grad_down, grad_down_bias)
    if not need_input:
        return layer_grads, None
    grad_hat = grad_normed * gain_row.astype(jnp.float32)
    grad_new = grad_h + hid_scale * (grad_hat - hid_hat * jnp.mean(grad_hat * hid_hat, axis=-1, keepdims=True))
    return layer_grads, grad_new


def solution(mesh):
    data_axis = mesh.axis_names[0]

    def device_grads(tokens, upstream, norm_gain, w_up, bias_up, w_down, bias_down):
        top_hidden, saved_acts = forward_stack(tokens, norm_gain, w_up, bias_up, w_down, bias_down)
        grad_h = top_gradient(top_hidden, upstream)
        num_layers = norm_gain.shape[0]
        reduced = [None] * num_layers
        for layer_idx in reversed(range(num_layers)):
            local_grads, grad_h = layer_backward(grad_h, saved_acts[layer_idx], norm_gain[layer_idx], w_up[layer_idx], w_down[layer_idx], layer_idx > 0)
            reduced[layer_idx] = lax.psum(local_grads, data_axis)
        return tuple(jnp.stack([reduced[layer_idx][which_grad] for layer_idx in range(num_layers)]) for which_grad in range(5))

    row_spec = P(data_axis, None)
    full_spec = P()
    return jax.shard_map(
        device_grads,
        mesh=mesh,
        in_specs=(row_spec, row_spec, full_spec, full_spec, full_spec, full_spec, full_spec),
        out_specs=(full_spec, full_spec, full_spec, full_spec, full_spec),
        check_vma=False,
    )
```

profile of v0, /device:TPU:0, one launch (start us, length us, event | category | flops | bytes accessed | tf_op | source)
XLA Modules:
  0.0 833.9 jit_solution(18182785000091155651)
XLA Ops:
  8.0 0.8 convert_reduce_fusion
  8.8 0.8 slice_convert_fusion
  9.6 3.2 copy.12
  13.5 1.1 copy-done
  14.6 3.2 copy.14
  17.8 16.3 %add_convert_fusion.1 = bf16[2048,3072]{1,0:T(8,128)(2,1)} fusion(f32[3072]{0:T(1024)S(1)} %bitcast.61, bf16[2,768,3072]{2,1,0:T(8,128)(2,1)} %param.10, bf16[2048,768]{0,1:T(8,128)(2,1)} %copy-done, f32[768]{0:T(1024)S(1)} %get-tuple-element.10, f32[2048]{0:T(1024)S(1)} %add_rsqrt_fusion.2), kind=kOutput, calls=%fused_computation.29 | convolution fusion | flops 9682550784 | bytes 20470784 | tf_op jit(solution)/shard_map/dot_general | solution.py:26
  34.1 19.0 %fusion.39 = (f32[2048]{0:T(1024)S(1)}, bf16[2048,768]{0,1:T(8,128)(2,1)}) fusion(f32[768]{0:T(1024)S(1)} %get-tuple-element.8, bf16[2,3072,768]{2,1,0:T(8,128)(2,1)} %param.12, bf16[2048,3072]{1,0:T(8,128)(2,1)} %add_convert_fusion.1, bf16[2048,768]{0,1:T(8,128)(2,1)S(1)} %copy-done.1), kind=kOutput, calls=%fused_computation.63 | convolution fusion | flops 9737598976 | bytes 23604224 | tf_op jit(solution)/shard_map/dot_general | solution.py:28
  53.1 16.2 %add_convert_fusion = bf16[2048,3072]{1,0:T(8,128)(2,1)} fusion(f32[3072]{0:T(1024)S(1)} %bitcast.60, bf16[2,768,3072]{2,1,0:T(8,128)(2,1)} %param.10, bf16[2048,768]{0,1:T(8,128)(2,1)} %get-tuple-element.27, f32[768]{0:T(1024)S(1)} %get-tuple-element.9, f32[2048]{0:T(1024)S(1)} %add_rsqrt_fusion.1), kind=kOutput, calls=%fused_computation.28 | convolution fusion | flops 9682550784 | bytes 20470784 | tf_op jit(solution)/shard_map/dot_general | solution.py:26
  69.3 17.9 %fusion.27 = (f32[2048]{0:T(1024)S(1)}, bf16[2048,768]{0,1:T(8,128)(2,1)S(1)}) fusion(f32[768]{0:T(1024)S(1)} %get-tuple-element.7, bf16[2,3072,768]{2,1,0:T(8,128)(2,1)} %param.12, bf16[2048,3072]{1,0:T(8,128)(2,1)} %add_convert_fusion, bf16[2048,768]{0,1:T(8,128)(2,1)} %get-tuple-element.27), kind=kOutput, calls=%fused_computation.51 | convolution fusion | flops 9737598976 | bytes 23604224 | tf_op jit(solution)/shard_map/dot_general | solution.py:28
  87.2 1.4 fusion.28
  88.5 23.0 %convolution_bitcast_fusion = f32[1,3072,768]{2,1,0:T(8,128)} fusion(bf16[2048,768]{0,1:T(8,128)(2,1)S(1)} %get-tuple-element.29, bf16[2048,768]{0,1:T(8,128)(2,1)S(1)} %copy.14, f32[2048]{0:T(1024)S(1)} %broadcast_multiply_fusion.1, f32[2048]{0:T(1024)S(1)} %add_rsqrt_fusion, bf16[2048,3072]{1,0:T(8,128)(2,1)} %add_convert_fusion), kind=kOutput, calls=%fused_computation.74 | convolution fusion | flops 9737601024 | bytes 28327936 | tf_op jit(solution)/shard_map/dot_general | solution.py:45
  111.5 30.9 %fusion.104 = (f32[3072]{0:T(1024)}, bf16[2048,3072]{1,0:T(8,128)(2,1)}) fusion(bf16[2048,3072]{1,0:T(8,128)(2,1)} %add_convert_fusion, bf16[2,3072,768]{2,1,0:T(8,128)(2,1)} %param.12, bf16[2048,768]{0,1:T(8,128)(2,1)S(1)} %get-tuple-element.29, bf16[2048,768]{0,1:T(8,128)(2,1)S(1)} %copy.14, f32[2048]{0:T(1024)S(1)} %broadcast_multiply_fusion.1, ...), kind=kOutput, calls=%fused_computation.117 | convolution fusion | flops 9813095424 | bytes 36204544 | tf_op jit(solution)/shard_map/dot_general | solution.py:47
  142.4 15.1 %fusion.34 = (f32[2048]{0:T(1024)S(1)}, f32[768]{0:T(1024)S(1)}, f32[2048,768]{0,1:T(8,128)S(1)}) fusion(bf16[2048,768]{0,1:T(8,128)(2,1)S(1)} %copy-done.5, f32[768]{0:T(1024)S(1)} %get-tuple-element.9, f32[2048]{0:T(1024)S(1)} %add_rsqrt_fusion.1, bf16[2,768,3072]{2,1,0:T(8,128)(2,1)} %param.10, bf16[2048,3072]{1,0:T(8,128)(2,1)} %get-tuple-element.32), kind=kOutput, calls=%fused_computation.58 | convolution fusion | flops 9674683392 | bytes 26761216 | tf_op jit(solution)/shard_map/dot_general | solution.py:53
  157.5 15.4 %fusion.50 = f32[1,768,3072]{2,1,0:T(8,128)} fusion(bf16[2048,3072]{1,0:T(8,128)(2,1)} %get-tuple-element.32, bf16[2048,768]{0,1:T(8,128)(2,1)S(1)} %copy-done.5, f32[768]{0:T(1024)S(1)} %get-tuple-element.9, f32[2048]{0:T(1024)S(1)} %add_rsqrt_fusion.1), kind=kOutput, calls=%fused_computation.76 | convolution fusion | flops 9669967872 | bytes 25177088 | tf_op jit(solution)/shard_map/dot_general | solution.py:51
  173.0 5.2 fusion.102
  178.1 23.0 %convolution_bitcast_fusion.1 = f32[1,3072,768]{2,1,0:T(8,128)} fusion(bf16[2048,768]{0,1:T(8,128)(2,1)} %get-tuple-element.22, bf16[2048,3072]{1,0:T(8,128)(2,1)} %add_convert_fusion.1), kind=kOutput, calls=%fused_computation.75 | convolution fusion | flops 9726590976 | bytes 25165824 | tf_op jit(solution)/shard_map/dot_general | solution.py:45
  201.2 33.1 %fusion.105 = (f32[3072]{0:T(1024)S(1)}, bf16[2048,3072]{1,0:T(8,128)(2,1)}) fusion(bf16[2048,3072]{1,0:T(8,128)(2,1)} %add_convert_fusion.1, bf16[2,3072,768]{2,1,0:T(8,128)(2,1)S(1)} %bitcast.63, bf16[2048,768]{0,1:T(8,128)(2,1)S(1)} %copy-done.6), kind=kOutput, calls=%fused_computation.118 | convolution fusion | flops 9802085376 | bytes 33042432 | tf_op jit(solution)/shard_map/dot_general | solution.py:47
  234.4 15.2 %fusion.53 = f32[1,768,3072]{2,1,0:T(8,128)} fusion(bf16[2048,3072]{1,0:T(8,128)(2,1)} %get-tuple-element.34, bf16[2048,768]{0,1:T(8,128)(2,1)S(1)} %copy-done.2, f32[768]{0:T(1024)S(1)} %copy-done.11, f32[2048]{0:T(1024)S(1)} %copy-done.9), kind=kOutput, calls=%fused_computation.77 | convolution fusion | flops 9669967872 | bytes 25177088 | tf_op jit(solution)/shard_map/dot_general | solution.py:51
  249.6 14.6 %fusion.26 = f32[768]{0:T(1024)S(1)} fusion(bf16[2048,768]{0,1:T(8,128)(2,1)S(1)} %copy-done.2, f32[2048]{0:T(1024)S(1)} %copy-done.9, bf16[2,768,3072]{2,1,0:T(8,128)(2,1)} %param.10, bf16[2048,3072]{1,0:T(8,128)(2,1)} %get-tuple-element.34), kind=kOutput, calls=%fused_computation.50 | convolution fusion | flops 9669966848 | bytes 20458496 | tf_op jit(solution)/shard_map/dot_general | solution.py:53
  264.2 43.7 %all-reduce = (f32[1,768]{1,0:T(1,128)S(1)}, f32[1,768]{1,0:T(1,128)S(1)}, f32[1,3072]{1,0:T(1,128)S(1)}, f32[1,3072]{1,0:T(1,128)S(1)}, f32[1,768]{1,0:T(1,128)S(1)}, /*index=5*/f32[1,768]{1,0:T(1,128)S(1)}) all-reduce(f32[1,768]{1,0:T(1,128)S(1)} %stack.46, f32[1,768]{1,0:T(1,128)S(1)} %stack.45, ...), channel_id=1, replica_groups=mesh['data'=32] {'data'}, use_global_device_ids=true, to_apply=%region_8.0 | all-reduce | flops 9216 | bytes 73728 | tf_op jit(solution)/shard_map/psum | solution.py:73
  309.1 492.4 %all-reduce.4.cloned.1.call-done = (f32[1,768,3072]{2,1,0:T(8,128)}, f32[1,768,3072]{2,1,0:T(8,128)}, f32[1,3072,768]{2,1,0:T(8,128)}, f32[1,3072,768]{2,1,0:T(8,128)}) async-done(((f32[1,768,3072]{2,1,0:T(8,128)}, f32[1,768,3072]{2,1,0:T(8,128)}, f32[1,3072,768]{2,1,0:T(8,128)}, f32[1,3072,768]{2,1,0:T(8,128)}), (f32[1,768,3072]{2,1,0:T(8,128)}, f32[1,768,3072]{2,1,0:T(8,128)}, f32[1,3072,768]{2,1,0:T(8,128)}, ...) | async-done | bytes 37748752 | tf_op jit(solution)/shard_map/psum | solution.py:73
  801.6 14.9 %pad_maximum_fusion = f32[2,768,3072]{2,1,0:T(8,128)} fusion(f32[1,768,3072]{2,1,0:T(8,128)} %get-tuple-element.17, f32[1,768,3072]{2,1,0:T(8,128)} %get-tuple-element.18), kind=kLoop, calls=%fused_computation.30 | loop fusion | flops 4718592 | bytes 37748736 | tf_op jit(solution)/shard_map/stack | solution.py:74
  816.8 3.1 copy-done.4
  819.9 6.9 pad_maximum_fusion.1
  (44 shorter events, 3.2 us)
Async XLA Ops:
  7.2 794.4 %all-reduce.4.cloned.1.call-start = ((), (), s32[]{:S(2)}) async-start(), calls=%async_computation | async-start | bytes 75497472 | tf_op jit(solution)/shard_map/psum | solution.py:73
  8.0 26.1 %copy-start.10 = (f32[768]{0:T(1024)}, f32[768]{0:T(1024)S(1)}, u32[]{:S(2)}) copy-start(f32[768]{0:T(1024)S(1)} %get-tuple-element.10) | copy-start | bytes 9220
  12.8 1.8 copy-start
  14.6 19.5 %copy-start.8 = (f32[2048]{0:T(1024)}, f32[2048]{0:T(1024)S(1)}, u32[]{:S(2)}) copy-start(f32[2048]{0:T(1024)S(1)} %add_rsqrt_fusion.2) | copy-start | bytes 24580
  17.8 16.3 %copy-start.1 = (bf16[2048,768]{0,1:T(8,128)(2,1)S(1)}, bf16[2048,768]{0,1:T(8,128)(2,1)}, u32[]{:S(2)}) copy-start(bf16[2048,768]{0,1:T(8,128)(2,1)} %copy-done) | copy-start | bytes 9437188
  111.5 30.9 %copy-start.5 = (bf16[2048,768]{0,1:T(8,128)(2,1)S(1)}, bf16[2048,768]{0,1:T(8,128)(2,1)}, u32[]{:S(2)}) copy-start(bf16[2048,768]{0,1:T(8,128)(2,1)} %get-tuple-element.27) | copy-start | bytes 9437188
  173.0 28.2 %slice-start = ((s8[9437184]{0:T(1024)(128)(4,1)}), s8[1048576]{0:T(1024)(128)(4,1)S(1)}, s32[]{:S(2)}) async-start(s8[9437184]{0:T(1024)(128)(4,1)} %bitcast.62), calls=%async_computation.1 | async-start | bytes 2097152
  178.1 23.1 %copy-start.6 = (bf16[2048,768]{0,1:T(8,128)(2,1)S(1)}, bf16[2048,768]{0,1:T(8,128)(2,1)}, u32[]{:S(2)}) copy-start(bf16[2048,768]{0,1:T(8,128)(2,1)} %get-tuple-element.22) | copy-start | bytes 9437188
  178.1 23.1 %slice-start.1 = ((s8[9437184]{0:T(1024)(128)(4,1)}), s8[4194304]{0:T(1024)(128)(4,1)S(1)}, s32[]{:S(2)}) async-start(s8[9437184]{0:T(1024)(128)(4,1)} %bitcast.62), calls=%async_computation.2 | async-start | bytes 8388608
  178.1 23.1 %slice-start.2 = ((s8[9437184]{0:T(1024)(128)(4,1)}), s8[4194304]{0:T(1024)(128)(4,1)S(1)}, s32[]{:S(2)}) async-start(s8[9437184]{0:T(1024)(128)(4,1)} %bitcast.62), calls=%async_computation.3 | async-start | bytes 8388608
  201.2 33.2 %copy-start.2 = (bf16[2048,768]{0,1:T(8,128)(2,1)S(1)}, bf16[2048,768]{0,1:T(8,128)(2,1)}, u32[]{:S(2)}) copy-start(bf16[2048,768]{0,1:T(8,128)(2,1)} %copy-done) | copy-start | bytes 9437188
  201.2 33.2 %copy-start.9 = (f32[2048]{0:T(1024)S(1)}, f32[2048]{0:T(1024)}, u32[]{:S(2)}) copy-start(f32[2048]{0:T(1024)} %copy-done.8) | copy-start | bytes 24580
  201.2 33.2 %copy-start.11 = (f32[768]{0:T(1024)S(1)}, f32[768]{0:T(1024)}, u32[]{:S(2)}) copy-start(f32[768]{0:T(1024)} %copy-done.10) | copy-start | bytes 9220
  249.6 14.6 %copy-start.7 = (f32[3072]{0:T(1024)S(1)}, f32[3072]{0:T(1024)}, u32[]{:S(2)}) copy-start(f32[3072]{0:T(1024)} %get-tuple-element.31) | copy-start | bytes 36868
  801.6 15.2 %copy-start.3 = (f32[1,3072,768]{2,1,0:T(8,128)S(1)}, f32[1,3072,768]{2,1,0:T(8,128)}, u32[]{:S(2)}) copy-start(f32[1,3072,768]{2,1,0:T(8,128)} %get-tuple-element.19) | copy-start | bytes 28311556
  801.6 18.4 %copy-start.4 = (f32[1,3072,768]{2,1,0:T(8,128)S(1)}, f32[1,3072,768]{2,1,0:T(8,128)}, u32[]{:S(2)}) copy-start(f32[1,3072,768]{2,1,0:T(8,128)} %get-tuple-element.20) | copy-start | bytes 28311556
Sparse Core Ops, SparseCore 0:
  249.7 551.8 all-reduce.3
where the time goes:
time: 840 us; the launch traced here: 834 us
  waiting for transfers between devices  492 us (59%)
  matrix products  240 us (29%)
  blocking collectives  43.7 us (5%)
  other arithmetic  32.6 us (4%)
  between operations  14.5 us (2%)
  local copies, waits for them, and re-layouts  11 us (1%)
    psum x1, waiting for transfers between devices, device_grads(): reduced[layer_idx] = lax.psum(local_grads, data_axis)  492 us
    dot_general x2, matrix products, layer_backward(): lax.dot_general(grad_b, down_mat, FEATURE_DIMS, preferred_element_type=jn...  64 us
    dot_general x2, matrix products, layer_backward(): lax.dot_general(activated, grad_b, TOKEN_DIMS, preferred_element_type=jnp...  46 us
    psum x1, blocking collectives, device_grads(): reduced[layer_idx] = lax.psum(local_grads, data_axis)  43.7 us
    dot_general x2, matrix products, forward_stack(): jnp.dot(activated, w_down[layer_idx], preferred_element_type=jnp.float32)  36.9 us
    dot_general x2, matrix products, forward_stack(): jnp.dot(normed, w_up[layer_idx], preferred_element_type=jnp.float32)  32.5 us
    dot_general x2, matrix products, layer_backward(): lax.dot_general(normed, grad_pre_b, TOKEN_DIMS, preferred_element_type=jn...  30.6 us
    dot_general x2, matrix products, layer_backward(): lax.dot_general(grad_pre_b, up_mat, FEATURE_DIMS, preferred_element_type=...  29.6 us
  transfers between devices with their start and end apart: 1, of which 1 were waited for; matrix products, arithmetic and copies ran while one was open for 2% of the time, Pallas kernels for 0%

commit v1 on v0

--- a/solution.py
+++ b/solution.py
@@ -1,11 +1,22 @@
+import functools
+
 import jax
 import jax.numpy as jnp
 from jax import lax
+from jax.experimental import pallas as pl
+from jax.experimental.pallas import tpu as pltpu
 from jax.sharding import PartitionSpec as P
 
 EPSILON = 1e-6
 TOKEN_DIMS = (((0,), (0,)), ((), ()))
 FEATURE_DIMS = (((1,), (1,)), ((), ()))
+MESH = pl.DeviceIdType.MESH
+
+SET_ROWS = 64
+LAG = 2
+SLOTS = 8
+FIN_SLOTS = 16
+STAGES = 11
 
 
 def gelu_tanh(values):
@@ -60,6 +71,306 @@
     return layer_grads, grad_new
 
 
+def sum_kernel(axis, num_sets, per_mat, pd1, pu1, pd0, pu0, small, out_d, out_u, out_s,
+               acc, fin, land0, land1, land2, land3, land4, land5, send_sem, recv_sem, loc_sem):
+    width = acc.shape[2]
+    half = SET_ROWS // 2
+    piece = SET_ROWS // 8
+    me = lax.axis_index(axis)
+    core = lax.rem(me, 2)
+    x = lax.rem(me // 2, 2)
+    y = lax.rem(me // 4, 2)
+    z = me // 8
+    side = z // 2
+    inner = jnp.logical_or(z == 1, z == 2)
+    outer = jnp.logical_not(inner)
+    b1 = jnp.where(core == 0, x, y)
+    step1 = jnp.where(core == 0, 2, 4)
+    b2 = jnp.where(core == 0, y, x)
+    step2 = jnp.where(core == 0, 4, 2)
+    partner = me + 1 - 2 * core
+    near1 = me + step1 * (1 - 2 * b1)
+    near2 = me + step2 * (1 - 2 * b2)
+    zpair = me + 8 * (1 - 2 * lax.rem(z, 2))
+    zmid = me + 8 * (3 - 2 * z)
+
+    own_half = pl.multiple_of(b1 * half, 8)
+    far_half = pl.multiple_of((1 - b1) * half, 8)
+    start3 = pl.multiple_of(own_half + (1 - side) * piece, 8)
+    far2 = pl.multiple_of(own_half + (1 - side) * 2 * piece, 8)
+    near_2 = pl.multiple_of(own_half + side * 2 * piece, 8)
+    outer_piece = pl.multiple_of(own_half + side * 3 * piece, 8)
+    own_piece = pl.multiple_of(own_half + z * piece, 8)
+
+    barrier = pltpu.get_barrier_semaphore()
+    for peer in (partner, near1, near2, zpair):
+        pl.semaphore_signal(barrier, inc=1, device_id=(peer,), device_id_type=MESH)
+
+    @pl.when(inner)
+    def _():
+        pl.semaphore_signal(barrier, inc=1, device_id=(zmid,), device_id_type=MESH)
+
+    pl.semaphore_wait(barrier, jnp.where(inner, 5, 4))
+
+    def slot_of(k):
+        return lax.rem(k, SLOTS)
+
+    def copy_to(stage, k, src, dst, peer):
+        slot = slot_of(k)
+        return pltpu.make_async_remote_copy(
+            src_ref=src, dst_ref=dst, send_sem=send_sem.at[stage, slot], recv_sem=recv_sem.at[stage, slot],
+            device_id=(peer,), device_id_type=MESH)
+
+    def rows_of(k, base, n):
+        return acc.at[k, pl.ds(base, n), :]
+
+    def done_of(k, base, n):
+        return fin.at[lax.rem(k, FIN_SLOTS), pl.ds(base, n), :]
+
+    def add_rows(k, base, n, land):
+        acc[k, pl.ds(base, n), :] = acc[k, pl.ds(base, n), :] + land[slot_of(k)]
+
+    def place(mat, j, who):
+        if mat % 2 == 0:
+            return pl.ds(pl.multiple_of(j * 2 * SET_ROWS + who * SET_ROWS, SET_ROWS), SET_ROWS), pl.ds(0, width)
+        blocks = width // (2 * SET_ROWS)
+        col = pl.multiple_of((j // blocks) * width, width)
+        row = pl.multiple_of(lax.rem(j, blocks) * 2 * SET_ROWS + who * SET_ROWS, SET_ROWS)
+        return pl.ds(row, SET_ROWS), pl.ds(col, width)
+
+    def by_matrix(k, fn):
+        for mat in range(4):
+            @pl.when(jnp.logical_and(k >= mat * per_mat, k < (mat + 1) * per_mat))
+            def _(mat=mat):
+                fn(mat, k - mat * per_mat)
+
+        @pl.when(k >= 4 * per_mat)
+        def _():
+            fn(4, None)
+
+    def source(mat, j, who):
+        if mat == 4:
+            return small.at[pl.ds(pl.multiple_of(who * SET_ROWS, SET_ROWS), SET_ROWS), :]
+        rows, cols = place(mat, j, who)
+        return (pd1, pu1, pd0, pu0)[mat].at[rows, cols]
+
+    def target(mat, j, who):
+        if mat == 4:
+            return out_s.at[pl.ds(pl.multiple_of(who * SET_ROWS, SET_ROWS), SET_ROWS), :]
+        rows, cols = place(mat, j, who)
+        return (out_d if mat % 2 == 0 else out_u).at[1 - mat // 2, rows, cols]
+
+    def c_pair(k, mat=4, j=None):
+        return copy_to(0, k, source(mat, j, 1 - core), land0.at[slot_of(k)], partner)
+
+    def c_mine(k, mat=4, j=None):
+        return pltpu.make_async_copy(source(mat, j, core), acc.at[k], loc_sem.at[0, slot_of(k)])
+
+    def c_d1(k):
+        return copy_to(1, k, rows_of(k, far_half, half), land1.at[slot_of(k)], near1)
+
+    def c_za(k):
+        return copy_to(2, k, rows_of(k, start3, 3 * piece), land2.at[slot_of(k)], zpair)
+
+    def c_zb(k):
+        return copy_to(3, k, rows_of(k, far2, 2 * piece), land3.at[slot_of(k)], zmid)
+
+    def c_zc(k):
+        return copy_to(4, k, rows_of(k, outer_piece, piece), land4.at[slot_of(k)], zpair)
+
+    def c_d2(k):
+        return copy_to(5, k, rows_of(k, own_piece, piece), land5.at[slot_of(k)], near2)
+
+    def c_zd(k):
+        return copy_to(6, k, done_of(k, outer_piece, piece), done_of(k, outer_piece, piece), zpair)
+
+    def c_ze(k):
+        return copy_to(7, k, done_of(k, near_2, 2 * piece), done_of(k, near_2, 2 * piece), zmid)
+
+    def c_zf(k):
+        return copy_to(8, k, done_of(k, start3, 3 * piece), done_of(k, start3, 3 * piece), zpair)
+
+    def c_e1(k):
+        return copy_to(9, k, done_of(k, own_half, half), done_of(k, own_half, half), near1)
+
+    def c_out(k, mat=4, j=None):
+        return copy_to(10, k, done_of(k, 0, SET_ROWS), target(mat, j, core), partner)
+
+    def c_loc(k, mat=4, j=None):
+        return pltpu.make_async_copy(done_of(k, 0, SET_ROWS), target(mat, j, core), loc_sem.at[1, slot_of(k)])
+
+    def wait0(k):
+        pass
+
+    def send0(k):
+        def go(mat, j):
+            c_pair(k, mat, j).start()
+            c_mine(k, mat, j).start()
+        by_matrix(k, go)
+
+    def wait1(k):
+        c_pair(k).wait()
+        c_mine(k).wait()
+        add_rows(k, 0, SET_ROWS, land0)
+
+    def send1(k):
+        c_d1(k).start()
+
+    def wait2(k):
+        c_d1(k).wait()
+        add_rows(k, own_half, half, land1)
+
+    def send2(k):
+        @pl.when(outer)
+        def _():
+            c_za(k).start()
+
+    def wait3(k):
+        @pl.when(inner)
+        def _():
+            c_za(k).wait_recv()
+            add_rows(k, start3, 3 * piece, land2)
+
+        @pl.when(outer)
+        def _():
+            c_za(k).wait_send()
+
+    def send3(k):
+        @pl.when(inner)
+        def _():
+            c_zb(k).start()
+
+    def wait4(k):
+        @pl.when(inner)
+        def _():
+            c_zb(k).wait()
+            add_rows(k, near_2, 2 * piece, land3)
+
+    def send4(k):
+        @pl.when(inner)
+        def _():
+            c_zc(k).start()
+
+    def wait5(k):
+        @pl.when(inner)
+        def _():
+            c_zc(k).wait_send()
+
+        @pl.when(outer)
+        def _():
+            c_zc(k).wait_recv()
+            add_rows(k, outer_piece, piece, land4)
+
+    def send5(k):
+        c_d2(k).start()
+
+    def wait6(k):
+        c_d2(k).wait()
+        fin[lax.rem(k, FIN_SLOTS), pl.ds(own_piece, piece), :] = acc[k, pl.ds(own_piece, piece), :] + land5[slot_of(k)]
+
+    def send6(k):
+        @pl.when(outer)
+        def _():
+            c_zd(k).start()
+
+    def wait7(k):
+        @pl.when(inner)
+        def _():
+            c_zd(k).wait_recv()
+
+        @pl.when(outer)
+        def _():
+            c_zd(k).wait_send()
+
+    def send7(k):
+        @pl.when(inner)
+        def _():
+            c_ze(k).start()
+
+    def wait8(k):
+        @pl.when(inner)
+        def _():
+            c_ze(k).wait()
+
+    def send8(k):
+        @pl.when(inner)
+        def _():
+            c_zf(k).start()
+
+    def wait9(k):
+        @pl.when(inner)
+        def _():
+            c_zf(k).wait_send()
+
+        @pl.when(outer)
+        def _():
+            c_zf(k).wait_recv()
+
+    def send9(k):
+        c_e1(k).start()
+
+    def wait10(k):
+        c_e1(k).wait()
+
+    def send10(k):
+        def go(mat, j):
+            c_out(k, mat, j).start()
+            c_loc(k, mat, j).start()
+        by_matrix(k, go)
+
+    def wait11(k):
+        c_out(k).wait()
+        c_loc(k).wait()
+
+    def send11(k):
+        pass
+
+    waits = [wait0, wait1, wait2, wait3, wait4, wait5, wait6, wait7, wait8, wait9, wait10, wait11]
+    sends = [send0, send1, send2, send3, send4, send5, send6, send7, send8, send9, send10, send11]
+
+    def tick(t):
+        for stage in range(STAGES, -1, -1):
+            k = t - stage * LAG
+
+            @pl.when(jnp.logical_and(k >= 0, k < num_sets))
+            def _(k=k, stage=stage):
+                waits[stage](k)
+                sends[stage](k)
+
+    pl.loop(0, num_sets + STAGES * LAG)(tick)
+
+
+def sum_over_devices(axis, pd1, pu1, pd0, pu0, small):
+    hidden, width = pd1.shape
+    per_mat = hidden // (2 * SET_ROWS)
+    num_sets = 4 * per_mat + 1
+    piece = SET_ROWS // 8
+    any_spec = pl.BlockSpec(memory_space=pl.ANY)
+    f32 = jnp.float32
+    return pl.pallas_call(
+        functools.partial(sum_kernel, axis, num_sets, per_mat),
+        name="sum_over_devices",
+        out_shape=[jax.ShapeDtypeStruct((2, hidden, width), f32), jax.ShapeDtypeStruct((2, width, hidden), f32),
+                   jax.ShapeDtypeStruct(small.shape, f32)],
+        in_specs=[any_spec] * 5,
+        out_specs=[any_spec] * 3,
+        scratch_shapes=[
+            pltpu.VMEM((num_sets, SET_ROWS, width), f32),
+            pltpu.VMEM((FIN_SLOTS, SET_ROWS, width), f32),
+            pltpu.VMEM((SLOTS, SET_ROWS, width), f32),
+            pltpu.VMEM((SLOTS, SET_ROWS // 2, width), f32),
+            pltpu.VMEM((SLOTS, 3 * piece, width), f32),
+            pltpu.VMEM((SLOTS, 2 * piece, width), f32),
+            pltpu.VMEM((SLOTS, piece, width), f32),
+            pltpu.VMEM((SLOTS, piece, width), f32),
+            pltpu.SemaphoreType.DMA((STAGES, SLOTS)),
+            pltpu.SemaphoreType.DMA((STAGES, SLOTS)),
+            pltpu.SemaphoreType.DMA((2, SLOTS)),
+        ],
+        compiler_params=pltpu.CompilerParams(collective_id=0, has_side_effects=True, vmem_limit_bytes=40 * 1024 * 1024),
+    )(pd1, pu1, pd0, pu0, small)
+
+
 def solution(mesh):
     data_axis = mesh.axis_names[0]
 
@@ -67,11 +378,21 @@
         top_hidden, saved_acts = forward_stack(tokens, norm_gain, w_up, bias_up, w_down, bias_down)
         grad_h = top_gradient(top_hidden, upstream)
         num_layers = norm_gain.shape[0]
-        reduced = [None] * num_layers
+        grads = [None] * num_layers
         for layer_idx in reversed(range(num_layers)):
-            local_grads, grad_h = layer_backward(grad_h, saved_acts[layer_idx], norm_gain[layer_idx], w_up[layer_idx], w_down[layer_idx], layer_idx > 0)
-            reduced[layer_idx] = lax.psum(local_grads, data_axis)
-        return tuple(jnp.stack([reduced[layer_idx][which_grad] for layer_idx in range(num_layers)]) for which_grad in range(5))
+            grads[layer_idx], grad_h = layer_backward(grad_h, saved_acts[layer_idx], norm_gain[layer_idx], w_up[layer_idx], w_down[layer_idx], layer_idx > 0)
+        width = norm_gain.shape[1]
+        blocks = bias_up.shape[1] // width
+        rows = []
+        for layer_idx in range(num_layers):
+            gain, _, up_bias, _, down_bias = grads[layer_idx]
+            rows += [gain[None], up_bias.reshape(blocks, width), down_bias[None]]
+        small = jnp.concatenate(rows, axis=0)
+        small = jnp.pad(small, ((0, 2 * SET_ROWS - small.shape[0]), (0, 0)))
+        out_d, out_u, out_s = sum_over_devices(data_axis, grads[1][3], grads[1][1], grads[0][3], grads[0][1], small)
+        per = blocks + 2
+        layers = out_s[: num_layers * per].reshape(num_layers, per, width)
+        return (layers[:, 0], out_u, layers[:, 1 : 1 + blocks].reshape(num_layers, blocks * width), out_d, layers[:, 1 + blocks])
 
     row_spec = P(data_axis, None)
     full_spec = P()

time: 840 us -> 550 us (0.65)
  waiting for transfers between devices: 492 us -> 0 us
  Pallas kernels: 0 us -> 262 us
  blocking collectives: 43.7 us -> 0 us
  local copies, waits for them, and re-layouts: 11 us -> 38.3 us
  other arithmetic: 32.6 us -> 8.61 us
  between operations: 14.5 us -> 1.11 us
    psum x1 -> x0, waiting for transfers between devices: 492 us -> none  [device_grads(): reduced[layer_idx] = lax.psum(local_grads, data_axis)]
    pallas_call x0 -> x1, Pallas kernels: none -> 262 us  [sum_over_devices(): pl.pallas_call(functools.partial(sum_kernel, axis, num_sets, per_mat), na...]
    psum x1 -> x0, blocking collectives: 43.7 us -> none  [device_grads(): reduced[layer_idx] = lax.psum(local_grads, data_axis)]
    unnamed x32 -> x35, local copies, waits for them, and re-layouts: 11 us -> 37.5 us
    another operation x4 -> x0, other arithmetic: 23 us -> none  [device_grads(): jnp.stack([reduced[layer_idx][which_grad] for layer_idx in range(num_laye...]
  transfers between devices with their start and end apart: 1 -> 0, of which waited for: 1 -> 0; matrix products, arithmetic and copies ran while one was open for 2% -> 0% of each run, Pallas kernels for 0% -> 0%
where the time goes in v1:
time: 550 us; the launch traced here: 544 us
  Pallas kernels  262 us (48%)
  matrix products  234 us (43%)
  local copies, waits for them, and re-layouts  38.3 us (7%)
  other arithmetic  8.61 us (2%)
    pallas_call x1, Pallas kernels, sum_over_devices(): pl.pallas_call(functools.partial(sum_kernel, axis, num_sets, per_mat), na...  262 us
    dot_general x2, matrix products, layer_backward(): lax.dot_general(grad_b, down_mat, FEATURE_DIMS, preferred_element_type=jn...  61.2 us
    dot_general x2, matrix products, layer_backward(): lax.dot_general(activated, grad_b, TOKEN_DIMS, preferred_element_type=jnp...  45 us
    unnamed x35, local copies, waits for them, and re-layouts  37.5 us
    dot_general x2, matrix products, forward_stack(): jnp.dot(activated, w_down[layer_idx], preferred_element_type=jnp.float32)  37 us
    dot_general x2, matrix products, forward_stack(): jnp.dot(normed, w_up[layer_idx], preferred_element_type=jnp.float32)  32.5 us
    dot_general x2, matrix products, layer_backward(): lax.dot_general(grad_pre_b, up_mat, FEATURE_DIMS, preferred_element_type=...  30.4 us
    dot_general x2, matrix products, layer_backward(): lax.dot_general(normed, grad_pre_b, TOKEN_DIMS, preferred_element_type=jn...  28.2 us

profile of v1, /device:TPU:0, one launch (start us, length us, event | category | flops | bytes accessed | tf_op | source)
XLA Modules:
  0.0 544.5 jit_solution(5819462983327342344)
XLA Ops:
  1.4 0.8 convert_reduce_fusion
  2.2 0.8 slice_convert_fusion
  3.0 3.2 copy.20
  6.9 1.0 copy-done.4
  7.9 3.2 copy.22
  11.1 16.3 %add_convert_fusion.1 = bf16[2048,3072]{1,0:T(8,128)(2,1)} fusion(f32[3072]{0:T(1024)S(1)} %bitcast.57, bf16[2,768,3072]{2,1,0:T(8,128)(2,1)} %param.10, bf16[2048,768]{0,1:T(8,128)(2,1)} %copy-done.4, f32[768]{0:T(1024)S(1)} %get-tuple-element.14, f32[2048]{0:T(1024)S(1)} %add_rsqrt_fusion.2), kind=kOutput, calls=%fused_computation.29 | convolution fusion | flops 9682550784 | bytes 20470784 | tf_op jit(solution)/shard_map/dot_general | solution.py:37
  27.4 18.8 %fusion.39 = (f32[2048]{0:T(1024)S(1)}, bf16[2048,768]{0,1:T(8,128)(2,1)}) fusion(f32[768]{0:T(1024)S(1)} %get-tuple-element.16, bf16[2,3072,768]{2,1,0:T(8,128)(2,1)} %param.12, bf16[2048,3072]{1,0:T(8,128)(2,1)} %add_convert_fusion.1, bf16[2048,768]{0,1:T(8,128)(2,1)S(1)} %copy-done.5), kind=kOutput, calls=%fused_computation.61 | convolution fusion | flops 9737598976 | bytes 23604224 | tf_op jit(solution)/shard_map/dot_general | solution.py:39
  46.2 16.2 %add_convert_fusion = bf16[2048,3072]{1,0:T(8,128)(2,1)} fusion(f32[3072]{0:T(1024)S(1)} %bitcast.56, bf16[2,768,3072]{2,1,0:T(8,128)(2,1)} %param.10, bf16[2048,768]{0,1:T(8,128)(2,1)} %get-tuple-element.25, f32[768]{0:T(1024)S(1)} %get-tuple-element.13, f32[2048]{0:T(1024)S(1)} %add_rsqrt_fusion.1), kind=kOutput, calls=%fused_computation.28 | convolution fusion | flops 9682550784 | bytes 20470784 | tf_op jit(solution)/shard_map/dot_general | solution.py:37
  62.4 18.2 %fusion.27 = (f32[2048]{0:T(1024)S(1)}, bf16[2048,768]{0,1:T(8,128)(2,1)S(1)}) fusion(f32[768]{0:T(1024)S(1)} %get-tuple-element.15, bf16[2,3072,768]{2,1,0:T(8,128)(2,1)} %param.12, bf16[2048,3072]{1,0:T(8,128)(2,1)} %add_convert_fusion, bf16[2048,768]{0,1:T(8,128)(2,1)} %get-tuple-element.25), kind=kOutput, calls=%fused_computation.49 | convolution fusion | flops 9737598976 | bytes 23604224 | tf_op jit(solution)/shard_map/dot_general | solution.py:39
  80.6 1.4 fusion.28
  82.0 22.9 %fusion.92.pd1 = f32[3072,768]{1,0:T(8,128)} fusion(bf16[2048,768]{0,1:T(8,128)(2,1)S(1)} %get-tuple-element.27, bf16[2048,768]{0,1:T(8,128)(2,1)S(1)} %copy.22, f32[2048]{0:T(1024)S(1)} %broadcast_multiply_fusion.1, f32[2048]{0:T(1024)S(1)} %add_rsqrt_fusion, bf16[2048,3072]{1,0:T(8,128)(2,1)} %add_convert_fusion), kind=kOutput, calls=%fused_computation.97 | convolution fusion | flops 9737601024 | bytes 28327936 | tf_op jit(solution)/shard_map/dot_general | solution.py:56
  104.9 29.9 %fusion.102 = (f32[3072]{0:T(1024)S(1)}, bf16[2048,3072]{1,0:T(8,128)(2,1)}) fusion(bf16[2048,3072]{1,0:T(8,128)(2,1)} %add_convert_fusion, bf16[2,3072,768]{2,1,0:T(8,128)(2,1)} %param.12, bf16[2048,768]{0,1:T(8,128)(2,1)S(1)} %get-tuple-element.27, bf16[2048,768]{0,1:T(8,128)(2,1)S(1)} %copy.22, f32[2048]{0:T(1024)S(1)} %broadcast_multiply_fusion.1, ...), kind=kOutput, calls=%fused_computation.115 | convolution fusion | flops 9813095424 | bytes 36204544 | tf_op jit(solution)/shard_map/dot_general | solution.py:58
  135.4 15.6 %fusion.38 = (f32[768]{0:T(1024)S(1)}, f32[2048]{0:T(1024)S(1)}, f32[2048,768]{0,1:T(8,128)S(1)}) fusion(bf16[2048,768]{0,1:T(8,128)(2,1)} %get-tuple-element.25, f32[2048]{0:T(1024)S(1)} %add_rsqrt_fusion.1, f32[768]{0:T(1024)S(1)} %get-tuple-element.13, bf16[2,768,3072]{2,1,0:T(8,128)(2,1)} %param.10, bf16[2048,3072]{1,0:T(8,128)(2,1)} %get-tuple-element.32), kind=kOutput, calls=%fused_computation.60 | convolution fusion | flops 9674683392 | bytes 26761216 | tf_op jit(solution)/shard_map/dot_general | solution.py:64
  151.1 15.8 %fusion.48.pu1 = f32[768,3072]{1,0:T(8,128)} fusion(bf16[2048,3072]{1,0:T(8,128)(2,1)} %get-tuple-element.32, bf16[2048,768]{0,1:T(8,128)(2,1)S(1)} %copy-done.7, f32[768]{0:T(1024)S(1)} %get-tuple-element.13, f32[2048]{0:T(1024)S(1)} %add_rsqrt_fusion.1), kind=kOutput, calls=%fused_computation.70 | convolution fusion | flops 9669967872 | bytes 25177088 | tf_op jit(solution)/shard_map/dot_general | solution.py:62
  166.9 4.2 fusion.98
  171.1 22.0 %fusion.85.pd0 = f32[3072,768]{1,0:T(8,128)} fusion(bf16[2048,768]{0,1:T(8,128)(2,1)S(1)} %get-tuple-element.18, bf16[2048,3072]{1,0:T(8,128)(2,1)} %add_convert_fusion.1), kind=kOutput, calls=%fused_computation.95 | convolution fusion | flops 9726590976 | bytes 25165824 | tf_op jit(solution)/shard_map/dot_general | solution.py:56
  193.1 31.4 %fusion.101 = (f32[3072]{0:T(1024)S(1)}, bf16[2048,3072]{1,0:T(8,128)(2,1)}) fusion(bf16[2048,3072]{1,0:T(8,128)(2,1)} %add_convert_fusion.1, bf16[2,3072,768]{2,1,0:T(8,128)(2,1)} %param.12, bf16[2048,768]{0,1:T(8,128)(2,1)S(1)} %get-tuple-element.18), kind=kOutput, calls=%fused_computation.114 | convolution fusion | flops 9802085376 | bytes 33042432 | tf_op jit(solution)/shard_map/dot_general | solution.py:58
  224.6 14.8 %fusion.26 = f32[768]{0:T(1024)S(1)} fusion(bf16[2048,768]{0,1:T(8,128)(2,1)S(1)} %copy-done.6, f32[2048]{0:T(1024)S(1)} %copy-done.10, bf16[2,768,3072]{2,1,0:T(8,128)(2,1)} %param.10, bf16[2048,3072]{1,0:T(8,128)(2,1)} %get-tuple-element.30), kind=kOutput, calls=%fused_computation.48 | convolution fusion | flops 9669966848 | bytes 20458496 | tf_op jit(solution)/shard_map/dot_general | solution.py:64
  239.4 12.4 %fusion.44.pu0 = f32[768,3072]{1,0:T(8,128)} fusion(bf16[2048,3072]{1,0:T(8,128)(2,1)S(1)} %copy-done.13, bf16[2048,768]{0,1:T(8,128)(2,1)S(1)} %copy-done.6, f32[768]{0:T(1024)S(1)} %copy-done.12, f32[2048]{0:T(1024)S(1)} %copy-done.10), kind=kOutput, calls=%fused_computation.66 | convolution fusion | flops 9669967872 | bytes 25177088 | tf_op jit(solution)/shard_map/dot_general | solution.py:62
  252.0 3.7 copy-done
  255.7 262.0 %sum_over_devices.1 = (f32[2,3072,768]{2,1,0:T(8,128)}, f32[2,768,3072]{2,1,0:T(8,128)}, f32[128,768]{1,0:T(8,128)S(1)}) custom-call(f32[3072,768]{1,0:T(8,128)S(1)} %copy-done, f32[768,3072]{1,0:T(8,128)} %fusion.48.pu1, f32[3072,768]{1,0:T(8,128)} %fusion.85.pd0, f32[768,3072]{1,0:T(8,128)} %fusion.44.pu0, f32[128,768]{1,0:T(8,128)S(1)} %pad.4.small), custom_call_target="tpu_custom_call" | custom-call | tf_op jit(solution)/shard_map/sum_over_devices/pallas_call | solution.py:350
  519.0 14.0 %copy.36 = f32[2,768,3072]{2,1,0:T(8,128)} copy(f32[2,768,3072]{2,1,0:T(8,128)} %get-tuple-element.48) | data formatting | bytes 37748736
  533.0 4.4 copy-done.1
  537.4 6.8 %copy.37 = f32[2,3072,768]{2,1,0:T(8,128)} copy(f32[2,3072,768]{2,1,0:T(8,128)S(1)} %copy-done.1) | data formatting | bytes 37748736
  (46 shorter events, 3.6 us)
Async XLA Ops:
  1.4 26.0 %copy-start.11 = (f32[768]{0:T(1024)}, f32[768]{0:T(1024)S(1)}, u32[]{:S(2)}) copy-start(f32[768]{0:T(1024)S(1)} %get-tuple-element.14) | copy-start | bytes 9220
  6.2 1.6 copy-start.4
  7.9 19.5 %copy-start.9 = (f32[2048]{0:T(1024)}, f32[2048]{0:T(1024)S(1)}, u32[]{:S(2)}) copy-start(f32[2048]{0:T(1024)S(1)} %add_rsqrt_fusion.2) | copy-start | bytes 24580
  11.1 16.3 %copy-start.5 = (bf16[2048,768]{0,1:T(8,128)(2,1)S(1)}, bf16[2048,768]{0,1:T(8,128)(2,1)}, u32[]{:S(2)}) copy-start(bf16[2048,768]{0,1:T(8,128)(2,1)} %copy-done.4) | copy-start | bytes 9437188
  80.6 24.3 %copy-start.2 = (bf16[2048,768]{0,1:T(8,128)(2,1)}, bf16[2048,768]{0,1:T(8,128)(2,1)S(1)}, u32[]{:S(2)}) copy-start(bf16[2048,768]{0,1:T(8,128)(2,1)S(1)} %get-tuple-element.27) | copy-start | bytes 9437188
  135.4 15.6 %copy-start.7 = (bf16[2048,768]{0,1:T(8,128)(2,1)S(1)}, bf16[2048,768]{0,1:T(8,128)(2,1)}, u32[]{:S(2)}) copy-start(bf16[2048,768]{0,1:T(8,128)(2,1)} %get-tuple-element.25) | copy-start | bytes 9437188
  151.1 15.8 %copy-start.3 = (bf16[2048,768]{0,1:T(8,128)(2,1)S(1)}, bf16[2048,768]{0,1:T(8,128)(2,1)}, u32[]{:S(2)}) copy-start(bf16[2048,768]{0,1:T(8,128)(2,1)} %copy-done.2) | copy-start | bytes 9437188
  193.1 31.4 %copy-start.6 = (bf16[2048,768]{0,1:T(8,128)(2,1)S(1)}, bf16[2048,768]{0,1:T(8,128)(2,1)}, u32[]{:S(2)}) copy-start(bf16[2048,768]{0,1:T(8,128)(2,1)} %copy-done.4) | copy-start | bytes 9437188
  193.1 31.4 %copy-start.10 = (f32[2048]{0:T(1024)S(1)}, f32[2048]{0:T(1024)}, u32[]{:S(2)}) copy-start(f32[2048]{0:T(1024)} %copy-done.9) | copy-start | bytes 24580
  224.5 14.8 %copy-start.12 = (f32[768]{0:T(1024)S(1)}, f32[768]{0:T(1024)}, u32[]{:S(2)}) copy-start(f32[768]{0:T(1024)} %copy-done.11) | copy-start | bytes 9220
  224.5 14.8 %copy-start.13 = (bf16[2048,3072]{1,0:T(8,128)(2,1)S(1)}, bf16[2048,3072]{1,0:T(8,128)(2,1)}, u32[]{:S(2)}) copy-start(bf16[2048,3072]{1,0:T(8,128)(2,1)} %get-tuple-element.30) | copy-start | bytes 37748740
  239.4 12.4 %copy-start.8 = (f32[4,768]{1,0:T(4,128)S(1)}, f32[4,768]{1,0:T(4,128)}, u32[]{:S(2)}) copy-start(f32[4,768]{1,0:T(4,128)} %reshape.55) | copy-start | bytes 36868
  252.0 3.7 copy-start
  519.0 18.4 %copy-start.1 = (f32[2,3072,768]{2,1,0:T(8,128)S(1)}, f32[2,3072,768]{2,1,0:T(8,128)}, u32[]{:S(2)}) copy-start(f32[2,3072,768]{2,1,0:T(8,128)} %get-tuple-element.50) | copy-start | bytes 56623108

commit v2 on v1

v2 whole, which is shorter than its diff:
```python
import functools

import jax
import jax.numpy as jnp
from jax import lax
from jax.experimental import pallas as pl
from jax.experimental.pallas import tpu as pltpu
from jax.sharding import PartitionSpec as P

EPSILON = 1e-6
GELU_C = 0.7978845608028654
GELU_A = 0.044715
MESH = pl.DeviceIdType.MESH
bf16 = jnp.bfloat16
f32 = jnp.float32

ROW_TILE = 512
CHUNK = 512
SET_ROWS = 64
LAG = 2
SLOTS = 8
FIN_SLOTS = 16
STAGES = 11


def gelu_f32(u):
    inner = u * (GELU_C + (GELU_C * GELU_A) * (u * u))
    half = 0.5 * u
    return half + half * jnp.tanh(inner)


def forward_kernel(tok, up, gain, wu, bu, wd, bd, u_out, a_out, h_out, n_out, g_out, gb_out, hid):
    layer = pl.program_id(0)
    r = pl.program_id(1)
    rows = pl.ds(pl.multiple_of(r * ROW_TILE, ROW_TILE), ROW_TILE)

    @pl.when(layer == 0)
    def _():
        hid[rows, :] = tok[...]

    xb = hid[rows, :]
    x = xb.astype(f32)
    scale = lax.rsqrt(jnp.mean(x * x, axis=-1, keepdims=True) + EPSILON)
    n = ((x * scale) * gain[0].astype(f32)).astype(bf16)
    h_out[0] = xb
    n_out[0] = n
    hidden = wu.shape[2]
    acc = None
    for j in range(hidden // CHUNK):
        cols = pl.ds(j * CHUNK, CHUNK)
        pre = jnp.dot(n, wu[0, :, cols], preferred_element_type=f32) + bu[0, :, cols].astype(f32)
        u = pre.astype(bf16)
        u_out[0, :, cols] = u
        a = gelu_f32(u.astype(f32)).astype(bf16)
        a_out[0, :, cols] = a
        part = jnp.dot(a, wd[0, cols, :], preferred_element_type=f32)
        acc = part if acc is None else acc + part
    new = ((x + acc) + bd[0].astype(f32)).astype(bf16)
    hid[rows, :] = new

    @pl.when(layer == 1)
    def _():
        top = new.astype(f32)
        s = lax.rsqrt(jnp.mean(top * top, axis=-1, keepdims=True) + EPSILON)
        zt = top * s
        upf = up[...].astype(f32)
        g = s * (upf - zt * jnp.mean(upf * zt, axis=-1, keepdims=True))
        g_out[...] = g
        gb_out[...] = g.astype(bf16)


def forward(tokens, upstream, norm_gain, w_up, bias_up, w_down, bias_down):
    rows, width = tokens.shape
    layers, _, hidden = w_up.shape
    tm = ROW_TILE
    grid = (layers, rows // tm)
    return pl.pallas_call(
        forward_kernel,
        name="forward",
        grid=grid,
        in_specs=[
            pl.BlockSpec((tm, width), lambda l, r: (r * (1 - l), 0)),
            pl.BlockSpec((tm, width), lambda l, r: (r * l, 0)),
            pl.BlockSpec((1, 1, width), lambda l, r: (l, 0, 0)),
            pl.BlockSpec((1, width, hidden), lambda l, r: (l, 0, 0)),
            pl.BlockSpec((1, 1, hidden), lambda l, r: (l, 0, 0)),
            pl.BlockSpec((1, hidden, width), lambda l, r: (l, 0, 0)),
            pl.BlockSpec((1, 1, width), lambda l, r: (l, 0, 0)),
        ],
        out_specs=[
            pl.BlockSpec((1, tm, hidden), lambda l, r: (l, r, 0)),
            pl.BlockSpec((1, tm, hidden), lambda l, r: (l, r, 0)),
            pl.BlockSpec((1, tm, width), lambda l, r: (l, r, 0)),
            pl.BlockSpec((1, tm, width), lambda l, r: (l, r, 0)),
            pl.BlockSpec((tm, width), lambda l, r: (r * l, 0)),
            pl.BlockSpec((tm, width), lambda l, r: (r * l, 0)),
        ],
        out_shape=[
            jax.ShapeDtypeStruct((layers, rows, hidden), bf16),
            jax.ShapeDtypeStruct((layers, rows, hidden), bf16),
            jax.ShapeDtypeStruct((layers, rows, width), bf16),
            jax.ShapeDtypeStruct((layers, rows, width), bf16),
            jax.ShapeDtypeStruct((rows, width), f32),
            jax.ShapeDtypeStruct((rows, width), bf16),
        ],
        scratch_shapes=[pltpu.VMEM((rows, width), bf16)],
        compiler_params=pltpu.CompilerParams(vmem_limit_bytes=60 * 1024 * 1024, dimension_semantics=("arbitrary", "arbitrary")),
    )(tokens, upstream, norm_gain[:, None, :], w_up, bias_up[:, None, :], w_down, bias_down[:, None, :])


def backward_kernel(axis, num_sets, per_mat, g_hbm, gb_hbm, a_hbm, u_hbm, n_hbm, h_hbm, wd_hbm, wu_hbm, gain,
                    out_d, out_u, out_s, part_d, part_u, part_s,
                    acc, fin, land0, land1, land2, land3, land4, land5,
                    g, gb, m, xbuf, nbuf, hbuf, wd, wu, dbuf, rbuf, sbuf,
                    send_sem, recv_sem, loc_sem, x_sem, w_sem, r_sem, in_sem):
    width = acc.shape[2]
    half = SET_ROWS // 2
    piece = SET_ROWS // 8
    me = lax.axis_index(axis)
    core = lax.rem(me, 2)
    x = lax.rem(me // 2, 2)
    y = lax.rem(me // 4, 2)
    z = me // 8
    side = z // 2
    inner = jnp.logical_or(z == 1, z == 2)
    outer = jnp.logical_not(inner)
    b1 = jnp.where(core == 0, x, y)
    step1 = jnp.where(core == 0, 2, 4)
    b2 = jnp.where(core == 0, y, x)
    step2 = jnp.where(core == 0, 4, 2)
    partner = me + 1 - 2 * core
    near1 = me + step1 * (1 - 2 * b1)
    near2 = me + step2 * (1 - 2 * b2)
    zpair = me + 8 * (1 - 2 * lax.rem(z, 2))
    zmid = me + 8 * (3 - 2 * z)

    own_half = pl.multiple_of(b1 * half, 8)
    far_half = pl.multiple_of((1 - b1) * half, 8)
    start3 = pl.multiple_of(own_half + (1 - side) * piece, 8)
    far2 = pl.multiple_of(own_half + (1 - side) * 2 * piece, 8)
    near_2 = pl.multiple_of(own_half + side * 2 * piece, 8)
    outer_piece = pl.multiple_of(own_half + side * 3 * piece, 8)
    own_piece = pl.multiple_of(own_half + z * piece, 8)

    barrier = pltpu.get_barrier_semaphore()
    for peer in (partner, near1, near2, zpair):
        pl.semaphore_signal(barrier, inc=1, device_id=(peer,), device_id_type=MESH)

    @pl.when(inner)
    def _():
        pl.semaphore_signal(barrier, inc=1, device_id=(zmid,), device_id_type=MESH)

    pl.semaphore_wait(barrier, jnp.where(inner, 5, 4))

    def slot_of(k):
        return lax.rem(k, SLOTS)

    def copy_to(stage, k, src, dst, peer):
        slot = slot_of(k)
        return pltpu.make_async_remote_copy(
            src_ref=src, dst_ref=dst, send_sem=send_sem.at[stage, slot], recv_sem=recv_sem.at[stage, slot],
            device_id=(peer,), device_id_type=MESH)

    def rows_of(k, base, n):
        return acc.at[lax.rem(k, FIN_SLOTS), pl.ds(base, n), :]

    def done_of(k, base, n):
        return fin.at[lax.rem(k, FIN_SLOTS), pl.ds(base, n), :]

    def add_rows(k, base, n, land):
        slot = lax.rem(k, FIN_SLOTS)
        acc[slot, pl.ds(base, n), :] = acc[slot, pl.ds(base, n), :] + land[slot_of(k)]

    def place(kind, j, who):
        if kind == 0:
            return pl.ds(pl.multiple_of(j * 2 * SET_ROWS + who * SET_ROWS, SET_ROWS), SET_ROWS), pl.ds(0, width)
        blocks = width // (2 * SET_ROWS)
        col = pl.multiple_of((j // blocks) * width, width)
        row = pl.multiple_of(lax.rem(j, blocks) * 2 * SET_ROWS + who * SET_ROWS, SET_ROWS)
        return pl.ds(row, SET_ROWS), pl.ds(col, width)

    def by_matrix(k, fn):
        mat = k // per_mat
        j = lax.rem(k, per_mat)
        for kind in range(2):
            @pl.when(jnp.logical_and(mat < 4, lax.rem(mat, 2) == kind))
            def _(kind=kind):
                fn(kind, (1 - mat // 2, j))

        @pl.when(mat >= 4)
        def _():
            fn(2, None)

    def part_of(refs, kind, where, who):
        if kind == 2:
            return refs[2].at[pl.ds(pl.multiple_of(who * SET_ROWS, SET_ROWS), SET_ROWS), :]
        rows, cols = place(kind, where[1], who)
        return refs[kind].at[where[0], rows, cols]

    def source(kind, where, who):
        return part_of((part_d, part_u, part_s), kind, where, who)

    def target(kind, where, who):
        return part_of((out_d, out_u, out_s), kind, where, who)

    def c_pair(k, kind=2, where=None):
        return copy_to(0, k, source(kind, where, 1 - core), land0.at[slot_of(k)], partner)

    def c_mine(k, kind=2, where=None):
        return pltpu.make_async_copy(source(kind, where, core), acc.at[lax.rem(k, FIN_SLOTS)], loc_sem.at[0, slot_of(k)])

    def c_d1(k):
        return copy_to(1, k, rows_of(k, far_half, half), land1.at[slot_of(k)], near1)

    def c_za(k):
        return copy_to(2, k, rows_of(k, start3, 3 * piece), land2.at[slot_of(k)], zpair)

    def c_zb(k):
        return copy_to(3, k, rows_of(k, far2, 2 * piece), land3.at[slot_of(k)], zmid)

    def c_zc(k):
        return copy_to(4, k, rows_of(k, outer_piece, piece), land4.at[slot_of(k)], zpair)

    def c_d2(k):
        return copy_to(5, k, rows_of(k, own_piece, piece), land5.at[slot_of(k)], near2)

    def c_zd(k):
        return copy_to(6, k, done_of(k, outer_piece, piece), done_of(k, outer_piece, piece), zpair)

    def c_ze(k):
        return copy_to(7, k, done_of(k, near_2, 2 * piece), done_of(k, near_2, 2 * piece), zmid)

    def c_zf(k):
        return copy_to(8, k, done_of(k, start3, 3 * piece), done_of(k, start3, 3 * piece), zpair)

    def c_e1(k):
        return copy_to(9, k, done_of(k, own_half, half), done_of(k, own_half, half), near1)

    def c_out(k, kind=2, where=None):
        return copy_to(10, k, done_of(k, 0, SET_ROWS), target(kind, where, core), partner)

    def c_loc(k, kind=2, where=None):
        return pltpu.make_async_copy(done_of(k, 0, SET_ROWS), target(kind, where, core), loc_sem.at[1, slot_of(k)])

    def wait0(k):
        pass

    def send0(k):
        def go(kind, where):
            c_pair(k, kind, where).start()
            c_mine(k, kind, where).start()
        by_matrix(k, go)

    def wait1(k):
        c_pair(k).wait()
        c_mine(k).wait()
        add_rows(k, 0, SET_ROWS, land0)

    def send1(k):
        c_d1(k).start()

    def wait2(k):
        c_d1(k).wait()
        add_rows(k, own_half, half, land1)

    def send2(k):
        @pl.when(outer)
        def _():
            c_za(k).start()

    def wait3(k):
        @pl.when(inner)
        def _():
            c_za(k).wait_recv()
            add_rows(k, start3, 3 * piece, land2)

        @pl.when(outer)
        def _():
            c_za(k).wait_send()

    def send3(k):
        @pl.when(inner)
        def _():
            c_zb(k).start()

    def wait4(k):
        @pl.when(inner)
        def _():
            c_zb(k).wait()
            add_rows(k, near_2, 2 * piece, land3)

    def send4(k):
        @pl.when(inner)
        def _():
            c_zc(k).start()

    def wait5(k):
        @pl.when(inner)
        def _():
            c_zc(k).wait_send()

        @pl.when(outer)
        def _():
            c_zc(k).wait_recv()
            add_rows(k, outer_piece, piece, land4)

    def send5(k):
        c_d2(k).start()

    def wait6(k):
        c_d2(k).wait()
        slot = lax.rem(k, FIN_SLOTS)
        fin[slot, pl.ds(own_piece, piece), :] = acc[slot, pl.ds(own_piece, piece), :] + land5[slot_of(k)]

    def send6(k):
        @pl.when(outer)
        def _():
            c_zd(k).start()

    def wait7(k):
        @pl.when(inner)
        def _():
            c_zd(k).wait_recv()

        @pl.when(outer)
        def _():
            c_zd(k).wait_send()

    def send7(k):
        @pl.when(inner)
        def _():
            c_ze(k).start()

    def wait8(k):
        @pl.when(inner)
        def _():
            c_ze(k).wait()

    def send8(k):
        @pl.when(inner)
        def _():
            c_zf(k).start()

    def wait9(k):
        @pl.when(inner)
        def _():
            c_zf(k).wait_send()

        @pl.when(outer)
        def _():
            c_zf(k).wait_recv()

    def send9(k):
        c_e1(k).start()

    def wait10(k):
        c_e1(k).wait()

    def send10(k):
        def go(kind, where):
            c_out(k, kind, where).start()
            c_loc(k, kind, where).start()
        by_matrix(k, go)

    def wait11(k):
        c_out(k).wait()
        c_loc(k).wait()

    def send11(k):
        pass

    waits = [wait0, wait1, wait2, wait3, wait4, wait5, wait6, wait7, wait8, wait9, wait10, wait11]
    sends = [send0, send1, send2, send3, send4, send5, send6, send7, send8, send9, send10, send11]

    def tick(t):
        for stage in range(STAGES, -1, -1):
            k = t - stage * LAG

            @pl.when(jnp.logical_and(k >= 0, k < num_sets))
            def _(k=k, stage=stage):
                waits[stage](k)
                sends[stage](k)


    rows = g.shape[0]
    blocks = per_mat * 2 * SET_ROWS // width
    half_w = width // 2
    a_steps = 2 * blocks
    b_steps = 6 * blocks
    c_steps = 4
    layer_steps = a_steps + b_steps + c_steps
    all_steps = 2 * layer_steps
    tile = rows // 4
    small_rows = blocks + 2

    def load_x(q):
        layer = 1 - q // (2 * blocks)
        cols = pl.ds(pl.multiple_of(lax.rem(q, blocks) * width, width), width)
        for kind, ref in enumerate((a_hbm, u_hbm)):
            @pl.when(jnp.logical_and(q < 4 * blocks, lax.rem(q // blocks, 2) == kind))
            def _(ref=ref):
                pltpu.make_async_copy(ref.at[layer, :, cols], xbuf.at[lax.rem(q, 2)], x_sem.at[lax.rem(q, 2)]).start()

    def wait_x(q):
        pltpu.make_async_copy(a_hbm.at[0, :, pl.ds(0, width)], xbuf.at[lax.rem(q, 2)], x_sem.at[lax.rem(q, 2)]).wait()

    def w_copies(p):
        slot = lax.rem(p, 2)
        layer = 1 - p // blocks
        span = pl.ds(pl.multiple_of(lax.rem(p, blocks) * width, width), width)
        return (pltpu.make_async_copy(wd_hbm.at[layer, span, :], wd.at[slot], w_sem.at[0, slot]),
                pltpu.make_async_copy(wu_hbm.at[layer, :, span], wu.at[slot], w_sem.at[1, slot]))

    def layer_copies(layer):
        return (pltpu.make_async_copy(n_hbm.at[layer], nbuf, in_sem.at[2]), pltpu.make_async_copy(h_hbm.at[layer], hbuf, in_sem.at[3]))

    def result_wait(slot):
        pltpu.make_async_copy(rbuf.at[slot], part_d.at[0, pl.ds(0, half_w), :], r_sem.at[slot]).wait()

    load_gb = pltpu.make_async_copy(gb_hbm, gb, in_sem.at[0])
    load_g = pltpu.make_async_copy(g_hbm, g, in_sem.at[1])
    load_gb.start()
    load_x(jnp.int32(0))
    load_x(jnp.int32(1))
    for copy in w_copies(jnp.int32(0)):
        copy.start()
    load_g.start()
    sbuf[...] = jnp.zeros_like(sbuf)
    load_gb.wait()

    def step_a(layer, w, r):
        slot = lax.rem(w, 2)
        block = w // 2
        q = (1 - layer) * 2 * blocks + block

        @pl.when(w == 0)
        def _():
            for copy in layer_copies(layer):
                copy.start()
            m[...] = jnp.zeros_like(m)

        @pl.when(slot == 0)
        def _():
            wait_x(q)

        @pl.when(r >= 2)
        def _():
            result_wait(slot)

        cols = pl.ds(pl.multiple_of(slot * half_w, 128), half_w)
        rbuf[slot] = lax.dot_general(xbuf[lax.rem(q, 2), :, cols], gb[...], (((0,), (0,)), ((), ())), preferred_element_type=f32)
        out_rows = pl.ds(pl.multiple_of(w * half_w, 128), half_w)
        pltpu.make_async_copy(rbuf.at[slot], part_d.at[layer, out_rows, :], r_sem.at[slot]).start()

        @pl.when(slot == 1)
        def _():
            load_x(q + 2)

    def step_e(layer, block, i):
        q = (1 - layer) * 2 * blocks + blocks + block
        p = (1 - layer) * blocks + block

        @pl.when(i == 0)
        def _():
            wait_x(q)
            for copy in w_copies(p):
                copy.wait()

            @pl.when(p + 1 < 2 * blocks)
            def _():
                for copy in w_copies(p + 1):
                    copy.start()

        total = None
        for sub in range(2):
            span = pl.ds(pl.multiple_of((2 * i + sub) * tile, 16), tile)
            e = lax.dot_general(gb[span, :], wd[lax.rem(p, 2)], (((1,), (1,)), ((), ())), preferred_element_type=f32)
            u = xbuf[lax.rem(q, 2), span, :].astype(f32)
            sq = u * u
            t = jnp.tanh(u * (GELU_C + (GELU_C * GELU_A) * sq))
            slope = ((1.0 - t * t) * (0.5 * u)) * (GELU_C + (3.0 * GELU_C * GELU_A) * sq) + (0.5 + 0.5 * t)
            d = e * slope
            dbuf[span, :] = d.astype(bf16)
            col = jnp.sum(d, axis=0, keepdims=True)
            total = col if total is None else total + col
        row = pl.ds(layer * small_rows + 1 + block, 1)
        sbuf[row, :] = sbuf[row, :] + total

        @pl.when(i == 1)
        def _():
            load_x(q + 2)

    def step_m(layer, block, i):
        p = (1 - layer) * blocks + block
        span = pl.ds(pl.multiple_of(i * 2 * tile, 16), 2 * tile)
        m[span, :] = m[span, :] + lax.dot_general(dbuf[span, :], wu[lax.rem(p, 2)], (((1,), (1,)), ((), ())), preferred_element_type=f32)

    def step_u(layer, block, i):
        @pl.when(jnp.logical_and(block == 0, i == 0))
        def _():
            for copy in layer_copies(layer):
                copy.wait()

        result_wait(i)
        cols = pl.ds(pl.multiple_of(i * half_w, 128), half_w)
        rbuf[i] = lax.dot_general(nbuf[:, cols], dbuf[...], (((0,), (0,)), ((), ())), preferred_element_type=f32)
        out_cols = pl.ds(pl.multiple_of(block * width, width), width)
        pltpu.make_async_copy(rbuf.at[i], part_u.at[layer, cols, out_cols], r_sem.at[i]).start()

    def step_c(layer, i):
        @pl.when(jnp.logical_and(layer == 1, i == 0))
        def _():
            load_g.wait()

        span = pl.ds(pl.multiple_of(i * tile, 16), tile)
        x = hbuf[span, :].astype(f32)
        scale = lax.rsqrt(jnp.mean(x * x, axis=-1, keepdims=True) + EPSILON)
        hat = x * scale
        grad_n = m[span, :]
        old = g[span, :]
        gain_row = pl.ds(layer * small_rows, 1)
        bias_row = pl.ds(layer * small_rows + blocks + 1, 1)
        sbuf[gain_row, :] = sbuf[gain_row, :] + jnp.sum(grad_n * hat, axis=0, keepdims=True)
        sbuf[bias_row, :] = sbuf[bias_row, :] + jnp.sum(old, axis=0, keepdims=True)
        grad_hat = grad_n * gain[layer].astype(f32)
        new = old + scale * (grad_hat - hat * jnp.mean(grad_hat * hat, axis=-1, keepdims=True))
        g[span, :] = new
        gb[span, :] = new.astype(bf16)

    def compute(s):
        layer = 1 - s // layer_steps
        w = lax.rem(s, layer_steps)
        v = w - a_steps
        block = v // 6
        i = lax.rem(v, 2)
        what = lax.rem(v, 6) // 2
        r = (1 - layer) * 4 * blocks + w

        @pl.when(w < a_steps)
        def _():
            step_a(layer, w, r)

        in_b = jnp.logical_and(v >= 0, v < b_steps)
        for number, step in enumerate((step_e, step_m, step_u)):
            @pl.when(jnp.logical_and(in_b, what == number))
            def _(step=step):
                step(layer, block, i)

        @pl.when(v >= b_steps)
        def _():
            step_c(layer, v - b_steps)

    small_copy = pltpu.make_async_copy(sbuf, part_s, in_sem.at[4])

    def whole_step(s):
        @pl.when(s < all_steps)
        def _():
            compute(s)

        @pl.when(s == all_steps)
        def _():
            small_copy.start()
            result_wait(0)
            result_wait(1)
            small_copy.wait()

        @pl.when(s >= 2)
        def _():
            tick(s - 2)

    pl.loop(0, num_sets + STAGES * LAG + 2)(whole_step)


def backward(axis, g, gb, a, u, n, h, w_down, w_up, norm_gain):
    rows, width = g.shape
    hidden = a.shape[2]
    per_mat = hidden // (2 * SET_ROWS)
    num_sets = 4 * per_mat + 1
    piece = SET_ROWS // 8
    any_spec = pl.BlockSpec(memory_space=pl.ANY)
    shape = jax.ShapeDtypeStruct
    shapes = [shape((2, hidden, width), f32), shape((2, width, hidden), f32), shape((2 * SET_ROWS, width), f32)]
    return pl.pallas_call(
        functools.partial(backward_kernel, axis, num_sets, per_mat),
        name="backward_and_sum",
        out_shape=shapes + shapes,
        in_specs=[any_spec] * 8 + [pl.BlockSpec(memory_space=pltpu.VMEM)],
        out_specs=[any_spec] * 6,
        scratch_shapes=[
            pltpu.VMEM((FIN_SLOTS, SET_ROWS, width), f32),
            pltpu.VMEM((FIN_SLOTS, SET_ROWS, width), f32),
            pltpu.VMEM((SLOTS, SET_ROWS, width), f32),
            pltpu.VMEM((SLOTS, SET_ROWS // 2, width), f32),
            pltpu.VMEM((SLOTS, 3 * piece, width), f32),
            pltpu.VMEM((SLOTS, 2 * piece, width), f32),
            pltpu.VMEM((SLOTS, piece, width), f32),
            pltpu.VMEM((SLOTS, piece, width), f32),
            pltpu.VMEM((rows, width), f32),
            pltpu.VMEM((rows, width), bf16),
            pltpu.VMEM((rows, width), f32),
            pltpu.VMEM((2, rows, width), bf16),
            pltpu.VMEM((rows, width), bf16),
            pltpu.VMEM((rows, width), bf16),
            pltpu.VMEM((2, width, width), bf16),
            pltpu.VMEM((2, width, width), bf16),
            pltpu.VMEM((rows, width), bf16),
            pltpu.VMEM((2, width // 2, width), f32),
            pltpu.VMEM((2 * SET_ROWS, width), f32),
            pltpu.SemaphoreType.DMA((STAGES, SLOTS)),
            pltpu.SemaphoreType.DMA((STAGES, SLOTS)),
            pltpu.SemaphoreType.DMA((2, SLOTS)),
            pltpu.SemaphoreType.DMA((2,)),
            pltpu.SemaphoreType.DMA((2, 2)),
            pltpu.SemaphoreType.DMA((2,)),
            pltpu.SemaphoreType.DMA((5,)),
        ],
        compiler_params=pltpu.CompilerParams(collective_id=0, has_side_effects=True, vmem_limit_bytes=62 * 1024 * 1024),
    )(g, gb, a, u, n, h, w_down, w_up, norm_gain[:, None, :])


def solution(mesh):
    data_axis = mesh.axis_names[0]

    def device_grads(tokens, upstream, norm_gain, w_up, bias_up, w_down, bias_down):
        u, a, h, n, g, gb = forward(tokens, upstream, norm_gain, w_up, bias_up, w_down, bias_down)
        out_d, out_u, out_s = backward(data_axis, g, gb, a, u, n, h, w_down, w_up, norm_gain)[:3]
        num_layers, width = norm_gain.shape
        blocks = bias_up.shape[1] // width
        per = blocks + 2
        layers = out_s[: num_layers * per].reshape(num_layers, per, width)
        return (layers[:, 0], out_u, layers[:, 1 : 1 + blocks].reshape(num_layers, blocks * width), out_d, layers[:, 1 + blocks])

    row_spec = P(data_axis, None)
    full_spec = P()
    return jax.shard_map(
        device_grads,
        mesh=mesh,
        in_specs=(row_spec, row_spec, full_spec, full_spec, full_spec, full_spec, full_spec),
        out_specs=(full_spec, full_spec, full_spec, full_spec, full_spec),
        check_vma=False,
    )
```

time: 550 us -> 381 us (0.69); the launches traced: 544 us -> 381 us
  matrix products: 234 us -> 0 us
  Pallas kernels: 262 us -> 349 us
  other arithmetic: 8.61 us -> 0 us
  local copies, waits for them, and re-layouts: 38.3 us -> 31.2 us
    dot_general x12 -> x0, matrix products: 234 us -> none  [the longest x2 61.2 us: layer_backward(): lax.dot_general(grad_b, down_mat, FEATURE_DIMS, preferred_element_type=jn...]
    pallas_call x1 -> x2, Pallas kernels: 262 us -> 349 us  [the longest x1 288 us: backward(): pl.pallas_call(functools.partial(backward_kernel, axis, num_sets, per_mat...]
    unnamed x35 -> x7, local copies, waits for them, and re-layouts: 37.5 us -> 26.4 us
    reduce_sum x3 -> x0, other arithmetic: 6.21 us -> none  [the longest x1 4.19 us: layer_backward(): grad_down_bias = jnp.sum(grad_h, axis=0)]
where the time goes in v2:
time: 381 us
  Pallas kernels  349 us (92%)
  local copies, waits for them, and re-layouts  31.2 us (8%)
    pallas_call x1, Pallas kernels, backward(): pl.pallas_call(functools.partial(backward_kernel, axis, num_sets, per_mat...  288 us
    pallas_call x1, Pallas kernels, forward(): pl.pallas_call(forward_kernel, name='forward', grid=grid, in_specs=[pl.Bl...  61.6 us
    unnamed x7, local copies, waits for them, and re-layouts  26.4 us

profile of v2, /device:TPU:0, one launch (start us, length us, event | category | flops | bytes accessed | tf_op | source)
XLA Modules:
  0.0 381.0 jit_solution(9289960754864597713)
XLA Ops:
  0.6 1.3 copy.14.gain
  1.9 1.3 copy.16.bd
  3.2 1.3 copy.15.bu
  4.5 61.6 %forward.1 = (bf16[2,2048,3072]{2,1,0:T(8,128)(2,1)}, bf16[2,2048,3072]{2,1,0:T(8,128)(2,1)}, bf16[2,2048,768]{2,1,0:T(8,128)(2,1)}, bf16[2,2048,768]{2,1,0:T(8,...) custom-call(bf16[2048,768]{1,0:T(8,128)(2,1)} %tok.1, bf16[2048,768]{1,0:T(8,128)(2,1)} %up.1, ...), custom_call_target="tpu_custom_call" | custom-call | tf_op jit(solution)/shard_map/forward/pallas_call | solution.py:77
  66.1 287.7 %backward_and_sum.1 = (f32[2,3072,768]{2,1,0:T(8,128)}, f32[2,768,3072]{2,1,0:T(8,128)}, f32[128,768]{1,0:T(8,128)}, f32[2,3072,768]{2,1,0:T(8,128)}, f32[2,768,3072]{2,1,0:T(8,128)}, /*index=5*/f32[128,768]{1,0:T(8,128)}) custom-call(f32[2048,768]{1,0:T(8,128)} %get-tuple-element.14.g_hbm, bf16[2048,768]{1,0:T(8,128)(2,1)} %get-tuple-element.15.gb_hbm, ...), custom_call_target="tpu_custom_call" | custom-call | tf_op jit(solution)/shard_map/backward_and_sum/pallas_call | solution.py:583
  353.8 0.8 slice.12
  354.6 0.6 copy.20
  355.2 0.6 copy_bitcast_fusion
  355.8 0.0 copy-start
  355.8 14.0 %copy.25 = f32[2,768,3072]{2,1,0:T(8,128)} copy(f32[2,768,3072]{2,1,0:T(8,128)} %get-tuple-element.33) | data formatting | bytes 37748736
  369.8 4.4 %copy-done = f32[2,3072,768]{2,1,0:T(8,128)S(1)} copy-done((f32[2,3072,768]{2,1,0:T(8,128)S(1)}, f32[2,3072,768]{2,1,0:T(8,128)}, u32[]{:S(2)}) %copy-start) | copy-done | bytes 18874392
  374.2 6.8 %copy.26 = f32[2,3072,768]{2,1,0:T(8,128)} copy(f32[2,3072,768]{2,1,0:T(8,128)S(1)} %copy-done) | data formatting | bytes 37748736
  (3 shorter events, 0.0 us)
Async XLA Ops:
  355.8 18.4 %copy-start = (f32[2,3072,768]{2,1,0:T(8,128)S(1)}, f32[2,3072,768]{2,1,0:T(8,128)}, u32[]{:S(2)}) copy-start(f32[2,3072,768]{2,1,0:T(8,128)} %get-tuple-element.35) | copy-start | bytes 56623108

commit v3 on v2

--- a/solution.py
+++ b/solution.py
@@ -18,7 +18,7 @@
 CHUNK = 512
 SET_ROWS = 64
 LAG = 2
-SLOTS = 8
+SLOTS = 10
 FIN_SLOTS = 16
 STAGES = 11
 
@@ -29,6 +29,11 @@
     return half + half * jnp.tanh(inner)
 
 
+def row_of(ref, layer):
+    both = ref[...].astype(f32)
+    return jnp.where(layer == 0, both[0:1, :], both[1:2, :])
+
+
 def forward_kernel(tok, up, gain, wu, bu, wd, bd, u_out, a_out, h_out, n_out, g_out, gb_out, hid):
     layer = pl.program_id(0)
     r = pl.program_id(1)
@@ -41,21 +46,22 @@
     xb = hid[rows, :]
     x = xb.astype(f32)
     scale = lax.rsqrt(jnp.mean(x * x, axis=-1, keepdims=True) + EPSILON)
-    n = ((x * scale) * gain[0].astype(f32)).astype(bf16)
+    n = ((x * scale) * row_of(gain, layer)).astype(bf16)
+    bu_row = row_of(bu, layer)
     h_out[0] = xb
     n_out[0] = n
     hidden = wu.shape[2]
     acc = None
     for j in range(hidden // CHUNK):
         cols = pl.ds(j * CHUNK, CHUNK)
-        pre = jnp.dot(n, wu[0, :, cols], preferred_element_type=f32) + bu[0, :, cols].astype(f32)
+        pre = jnp.dot(n, wu[0, :, cols], preferred_element_type=f32) + bu_row[:, j * CHUNK : (j + 1) * CHUNK]
         u = pre.astype(bf16)
         u_out[0, :, cols] = u
         a = gelu_f32(u.astype(f32)).astype(bf16)
         a_out[0, :, cols] = a
         part = jnp.dot(a, wd[0, cols, :], preferred_element_type=f32)
         acc = part if acc is None else acc + part
-    new = ((x + acc) + bd[0].astype(f32)).astype(bf16)
+    new = ((x + acc) + row_of(bd, layer)).astype(bf16)
     hid[rows, :] = new
 
     @pl.when(layer == 1)
@@ -81,11 +87,11 @@
         in_specs=[
             pl.BlockSpec((tm, width), lambda l, r: (r * (1 - l), 0)),
             pl.BlockSpec((tm, width), lambda l, r: (r * l, 0)),
-            pl.BlockSpec((1, 1, width), lambda l, r: (l, 0, 0)),
+            pl.BlockSpec((layers, width), lambda l, r: (0, 0)),
             pl.BlockSpec((1, width, hidden), lambda l, r: (l, 0, 0)),
-            pl.BlockSpec((1, 1, hidden), lambda l, r: (l, 0, 0)),
+            pl.BlockSpec((layers, hidden), lambda l, r: (0, 0)),
             pl.BlockSpec((1, hidden, width), lambda l, r: (l, 0, 0)),
-            pl.BlockSpec((1, 1, width), lambda l, r: (l, 0, 0)),
+            pl.BlockSpec((layers, width), lambda l, r: (0, 0)),
         ],
         out_specs=[
             pl.BlockSpec((1, tm, hidden), lambda l, r: (l, r, 0)),
@@ -105,7 +111,7 @@
         ],
         scratch_shapes=[pltpu.VMEM((rows, width), bf16)],
         compiler_params=pltpu.CompilerParams(vmem_limit_bytes=60 * 1024 * 1024, dimension_semantics=("arbitrary", "arbitrary")),
-    )(tokens, upstream, norm_gain[:, None, :], w_up, bias_up[:, None, :], w_down, bias_down[:, None, :])
+    )(tokens, upstream, norm_gain, w_up, bias_up, w_down, bias_down)
 
 
 def backward_kernel(axis, num_sets, per_mat, g_hbm, gb_hbm, a_hbm, u_hbm, n_hbm, h_hbm, wd_hbm, wu_hbm, gain,
@@ -142,16 +148,6 @@
     outer_piece = pl.multiple_of(own_half + side * 3 * piece, 8)
     own_piece = pl.multiple_of(own_half + z * piece, 8)
 
-    barrier = pltpu.get_barrier_semaphore()
-    for peer in (partner, near1, near2, zpair):
-        pl.semaphore_signal(barrier, inc=1, device_id=(peer,), device_id_type=MESH)
-
-    @pl.when(inner)
-    def _():
-        pl.semaphore_signal(barrier, inc=1, device_id=(zmid,), device_id_type=MESH)
-
-    pl.semaphore_wait(barrier, jnp.where(inner, 5, 4))
-
     def slot_of(k):
         return lax.rem(k, SLOTS)
 
@@ -373,7 +369,7 @@
     sends = [send0, send1, send2, send3, send4, send5, send6, send7, send8, send9, send10, send11]
 
     def tick(t):
-        for stage in range(STAGES, -1, -1):
+        for stage in range(STAGES + 1):
             k = t - stage * LAG
 
             @pl.when(jnp.logical_and(k >= 0, k < num_sets))
@@ -386,7 +382,7 @@
     blocks = per_mat * 2 * SET_ROWS // width
     half_w = width // 2
     a_steps = 2 * blocks
-    b_steps = 6 * blocks
+    b_steps = 8 * blocks
     c_steps = 4
     layer_steps = a_steps + b_steps + c_steps
     all_steps = 2 * layer_steps
@@ -419,12 +415,22 @@
 
     load_gb = pltpu.make_async_copy(gb_hbm, gb, in_sem.at[0])
     load_g = pltpu.make_async_copy(g_hbm, g, in_sem.at[1])
+    load_x(jnp.int32(0))
     load_gb.start()
-    load_x(jnp.int32(0))
     load_x(jnp.int32(1))
     for copy in w_copies(jnp.int32(0)):
         copy.start()
     load_g.start()
+    barrier = pltpu.get_barrier_semaphore()
+    for peer in (partner, near1, near2, zpair):
+        pl.semaphore_signal(barrier, inc=1, device_id=(peer,), device_id_type=MESH)
+
+    @pl.when(inner)
+    def _():
+        pl.semaphore_signal(barrier, inc=1, device_id=(zmid,), device_id_type=MESH)
+
+    pl.semaphore_wait(barrier, jnp.where(inner, 5, 4))
+
     sbuf[...] = jnp.zeros_like(sbuf)
     load_gb.wait()
 
@@ -471,22 +477,19 @@
                 for copy in w_copies(p + 1):
                     copy.start()
 
-        total = None
-        for sub in range(2):
-            span = pl.ds(pl.multiple_of((2 * i + sub) * tile, 16), tile)
-            e = lax.dot_general(gb[span, :], wd[lax.rem(p, 2)], (((1,), (1,)), ((), ())), preferred_element_type=f32)
-            u = xbuf[lax.rem(q, 2), span, :].astype(f32)
-            sq = u * u
-            t = jnp.tanh(u * (GELU_C + (GELU_C * GELU_A) * sq))
-            slope = ((1.0 - t * t) * (0.5 * u)) * (GELU_C + (3.0 * GELU_C * GELU_A) * sq) + (0.5 + 0.5 * t)
-            d = e * slope
-            dbuf[span, :] = d.astype(bf16)
-            col = jnp.sum(d, axis=0, keepdims=True)
-            total = col if total is None else total + col
+        span = pl.ds(pl.multiple_of(i * tile, 16), tile)
+        e = lax.dot_general(gb[span, :], wd[lax.rem(p, 2)], (((1,), (1,)), ((), ())), preferred_element_type=f32)
+        u = xbuf[lax.rem(q, 2), span, :].astype(f32)
+        sq = u * u
+        t = jnp.tanh(u * (GELU_C + (GELU_C * GELU_A) * sq))
+        slope = ((1.0 - t * t) * (0.5 * u)) * (GELU_C + (3.0 * GELU_C * GELU_A) * sq) + (0.5 + 0.5 * t)
+        d = e * slope
+        dbuf[span, :] = d.astype(bf16)
+        total = jnp.sum(d, axis=0, keepdims=True)
         row = pl.ds(layer * small_rows + 1 + block, 1)
         sbuf[row, :] = sbuf[row, :] + total
 
-        @pl.when(i == 1)
+        @pl.when(i == 3)
         def _():
             load_x(q + 2)
 
@@ -522,7 +525,7 @@
         bias_row = pl.ds(layer * small_rows + blocks + 1, 1)
         sbuf[gain_row, :] = sbuf[gain_row, :] + jnp.sum(grad_n * hat, axis=0, keepdims=True)
         sbuf[bias_row, :] = sbuf[bias_row, :] + jnp.sum(old, axis=0, keepdims=True)
-        grad_hat = grad_n * gain[layer].astype(f32)
+        grad_hat = grad_n * row_of(gain, layer)
         new = old + scale * (grad_hat - hat * jnp.mean(grad_hat * hat, axis=-1, keepdims=True))
         g[span, :] = new
         gb[span, :] = new.astype(bf16)
@@ -531,9 +534,8 @@
         layer = 1 - s // layer_steps
         w = lax.rem(s, layer_steps)
         v = w - a_steps
-        block = v // 6
-        i = lax.rem(v, 2)
-        what = lax.rem(v, 6) // 2
+        block = v // 8
+        in_block = lax.rem(v, 8)
         r = (1 - layer) * 4 * blocks + w
 
         @pl.when(w < a_steps)
@@ -541,10 +543,10 @@
             step_a(layer, w, r)
 
         in_b = jnp.logical_and(v >= 0, v < b_steps)
-        for number, step in enumerate((step_e, step_m, step_u)):
-            @pl.when(jnp.logical_and(in_b, what == number))
-            def _(step=step):
-                step(layer, block, i)
+        for step, first, last in ((step_e, 0, 4), (step_m, 4, 6), (step_u, 6, 8)):
+            @pl.when(jnp.logical_and(in_b, jnp.logical_and(in_block >= first, in_block < last)))
+            def _(step=step, first=first):
+                step(layer, block, in_block - first)
 
         @pl.when(v >= b_steps)
         def _():
@@ -615,7 +617,79 @@
             pltpu.SemaphoreType.DMA((5,)),
         ],
         compiler_params=pltpu.CompilerParams(collective_id=0, has_side_effects=True, vmem_limit_bytes=62 * 1024 * 1024),
-    )(g, gb, a, u, n, h, w_down, w_up, norm_gain[:, None, :])
+    )(g, gb, a, u, n, h, w_down, w_up, norm_gain)
+
+
+OUT_RING = 8
+
+
+def emit_kernel(sum_d, sum_u, sum_s, gain_out, up_out, bias_up_out, down_out, bias_down_out, ring_d, ring_u, rows, sem_in, sem_out, sem_s):
+    layers, hidden, width = sum_d.shape
+    blocks = hidden // width
+    per = blocks + 2
+    small = pltpu.make_async_copy(sum_s.at[pl.ds(0, rows.shape[0]), :], rows, sem_s)
+    small.start()
+    down_rows = ring_d.shape[1]
+    up_rows = ring_u.shape[1]
+    jobs = []
+    for layer in range(layers):
+        for part in range(hidden // down_rows):
+            span = pl.ds(part * down_rows, down_rows)
+            jobs.append((sum_d.at[layer, span, :], ring_d, down_out.at[layer, span, :], 0))
+            span = pl.ds(part * up_rows, up_rows)
+            jobs.append((sum_u.at[layer, span, :], ring_u, up_out.at[layer, span, :], 1))
+    reads, writes = [], []
+    for number, (src, ring, dst, which) in enumerate(jobs):
+        slot = (number // 2) % OUT_RING
+        reads.append(pltpu.make_async_copy(src, ring.at[slot], sem_in.at[which, slot]))
+        writes.append(pltpu.make_async_copy(ring.at[slot], dst, sem_out.at[which, slot]))
+    ahead = 2 * OUT_RING
+    lead = ahead - 4
+    for number in range(min(lead, len(jobs))):
+        reads[number].start()
+    for number in range(len(jobs)):
+        reads[number].wait()
+        writes[number].start()
+        follow = number + lead
+        if follow < len(jobs):
+            if follow >= ahead:
+                writes[follow - ahead].wait()
+            reads[follow].start()
+        if number == 2:
+            small.wait()
+            for layer in range(layers):
+                base = layer * per
+                gain_out[layer : layer + 1, :] = rows[base : base + 1, :]
+                bias_down_out[layer : layer + 1, :] = rows[base + blocks + 1 : base + blocks + 2, :]
+                for block in range(blocks):
+                    bias_up_out[layer : layer + 1, block * width : (block + 1) * width] = rows[base + 1 + block : base + 2 + block, :]
+    for number in range(max(0, len(jobs) - ahead), len(jobs)):
+        writes[number].wait()
+
+
+def emit(sum_d, sum_u, sum_s):
+    layers, hidden, width = sum_d.shape
+    blocks = hidden // width
+    any_spec = pl.BlockSpec(memory_space=pl.ANY)
+    vmem_spec = pl.BlockSpec(memory_space=pltpu.VMEM)
+    shape = jax.ShapeDtypeStruct
+    return pl.pallas_call(
+        emit_kernel,
+        name="emit",
+        out_shape=[shape((layers, width), f32), shape((layers, width, hidden), f32), shape((layers, hidden), f32),
+                   shape((layers, hidden, width), f32), shape((layers, width), f32)],
+        in_specs=[any_spec] * 3,
+        out_specs=[vmem_spec, any_spec, vmem_spec, any_spec, vmem_spec],
+        scratch_shapes=[
+            pltpu.VMEM((OUT_RING, hidden // 8, width), f32),
+            pltpu.VMEM((OUT_RING, width // 8, hidden), f32),
+            pltpu.VMEM((8 * ((layers * (blocks + 2) + 7) // 8), width), f32),
+            pltpu.SemaphoreType.DMA((2, OUT_RING)),
+            pltpu.SemaphoreType.DMA((2, OUT_RING)),
+            pltpu.SemaphoreType.DMA,
+        ],
+        compiler_params=pltpu.CompilerParams(vmem_limit_bytes=60 * 1024 * 1024),
+    )(sum_d, sum_u, sum_s)
 
 
 def solution(mesh):
@@ -624,11 +698,7 @@
     def device_grads(tokens, upstream, norm_gain, w_up, bias_up, w_down, bias_down):
         u, a, h, n, g, gb = forward(tokens, upstream, norm_gain, w_up, bias_up, w_down, bias_down)
         out_d, out_u, out_s = backward(data_axis, g, gb, a, u, n, h, w_down, w_up, norm_gain)[:3]
-        num_layers, width = norm_gain.shape
-        blocks = bias_up.shape[1] // width
-        per = blocks + 2
-        layers = out_s[: num_layers * per].reshape(num_layers, per, width)
-        return (layers[:, 0], out_u, layers[:, 1 : 1 + blocks].reshape(num_layers, blocks * width), out_d, layers[:, 1 + blocks])
+        return tuple(emit(out_d, out_u, out_s))
 
     row_spec = P(data_axis, None)
     full_spec = P()

time: 381 us -> 360 us (0.945)
  local copies, waits for them, and re-layouts: 31.2 us -> 0 us
  Pallas kernels: 349 us -> 359 us
    unnamed x7 -> x0, local copies, waits for them, and re-layouts: 26.4 us -> none
    pallas_call x0 -> x1, Pallas kernels: none -> 25.6 us  [emit(): pl.pallas_call(emit_kernel, name='emit', out_shape=[shape((layers, width)...]
    pallas_call x1, Pallas kernels: 288 us -> 271 us  [backward(): pl.pallas_call(functools.partial(backward_kernel, axis, num_sets, per_mat...]
    broadcast_in_dim x3 -> x0, local copies, waits for them, and re-layouts: 3.9 us -> none  [the longest x1 1.33 us: forward(): bias_up[:, None, :]]
where the time goes in v3:
time: 360 us; the launch traced here: 359 us
  Pallas kernels  359 us (100%)
    pallas_call x1, Pallas kernels, backward(): pl.pallas_call(functools.partial(backward_kernel, axis, num_sets, per_mat...  271 us
    pallas_call x1, Pallas kernels, forward(): pl.pallas_call(forward_kernel, name='forward', grid=grid, in_specs=[pl.Bl...  61.7 us
    pallas_call x1, Pallas kernels, emit(): pl.pallas_call(emit_kernel, name='emit', out_shape=[shape((layers, width)...  25.6 us

profile of v3, /device:TPU:0, one launch (start us, length us, event | category | flops | bytes accessed | tf_op | source)
XLA Modules:
  0.0 359.3 jit_solution(10342037673049665486)
XLA Ops:
  0.6 61.7 %forward.1 = (bf16[2,2048,3072]{2,1,0:T(8,128)(2,1)}, bf16[2,2048,3072]{2,1,0:T(8,128)(2,1)}, bf16[2,2048,768]{2,1,0:T(8,128)(2,1)}, bf16[2,2048,768]{2,1,0:T(8,...) custom-call(bf16[2048,768]{1,0:T(8,128)(2,1)} %tok.1, bf16[2048,768]{1,0:T(8,128)(2,1)} %up.1, ...), custom_call_target="tpu_custom_call" | custom-call | tf_op jit(solution)/shard_map/forward/pallas_call | solution.py:83
  62.3 271.3 %backward_and_sum.1 = (f32[2,3072,768]{2,1,0:T(8,128)}, f32[2,768,3072]{2,1,0:T(8,128)}, f32[128,768]{1,0:T(8,128)}, f32[2,3072,768]{2,1,0:T(8,128)}, f32[2,768,3072]{2,1,0:T(8,128)}, /*index=5*/f32[128,768]{1,0:T(8,128)}) custom-call(f32[2048,768]{1,0:T(8,128)} %get-tuple-element.14.g_hbm, bf16[2048,768]{1,0:T(8,128)(2,1)} %get-tuple-element.15.gb_hbm, ...), custom_call_target="tpu_custom_call" | custom-call | tf_op jit(solution)/shard_map/backward_and_sum/pallas_call | solution.py:585
  333.6 25.6 %emit.1 = (f32[2,768]{1,0:T(2,128)}, f32[2,768,3072]{2,1,0:T(8,128)}, f32[2,3072]{1,0:T(2,128)}, f32[2,3072,768]{2,1,0:T(8,128)}, f32[2,768]{1,0:T(2,128)}) custom-call(f32[2,3072,768]{2,1,0:T(8,128)} %get-tuple-element.20.sum_d, f32[2,768,3072]{2,1,0:T(8,128)} %get-tuple-element.21.sum_u, f32[128,768]{1,0:T(8,128)} %get-tuple-element.22.sum_s), custom_call_target="tpu_custom_call" | custom-call | tf_op jit(solution)/shard_map/emit/pallas_call | solution.py:676

commit v4 on v3

--- a/solution.py
+++ b/solution.py
@@ -18,8 +18,8 @@
 CHUNK = 512
 SET_ROWS = 64
 LAG = 2
-SLOTS = 10
-FIN_SLOTS = 16
+SLOTS = 8
+FIN_SLOTS = 14
 STAGES = 11
 
 
@@ -115,9 +115,9 @@
 
 
 def backward_kernel(axis, num_sets, per_mat, g_hbm, gb_hbm, a_hbm, u_hbm, n_hbm, h_hbm, wd_hbm, wu_hbm, gain,
-                    out_d, out_u, out_s, part_d, part_u, part_s,
+                    out_d1, out_u1, out_v, out_s, part_d, part_u, part_s,
                     acc, fin, land0, land1, land2, land3, land4, land5,
-                    g, gb, m, xbuf, nbuf, hbuf, wd, wu, dbuf, rbuf, sbuf,
+                    gb, m, xbuf, nbuf, gtile, htile, wd, wu, dbuf, rbuf, sbuf,
                     send_sem, recv_sem, loc_sem, x_sem, w_sem, r_sem, in_sem):
     width = acc.shape[2]
     half = SET_ROWS // 2
@@ -178,32 +178,34 @@
     def by_matrix(k, fn):
         mat = k // per_mat
         j = lax.rem(k, per_mat)
-        for kind in range(2):
-            @pl.when(jnp.logical_and(mat < 4, lax.rem(mat, 2) == kind))
-            def _(kind=kind):
-                fn(kind, (1 - mat // 2, j))
-
-        @pl.when(mat >= 4)
-        def _():
-            fn(2, None)
-
-    def part_of(refs, kind, where, who):
-        if kind == 2:
-            return refs[2].at[pl.ds(pl.multiple_of(who * SET_ROWS, SET_ROWS), SET_ROWS), :]
-        rows, cols = place(kind, where[1], who)
-        return refs[kind].at[where[0], rows, cols]
-
-    def source(kind, where, who):
-        return part_of((part_d, part_u, part_s), kind, where, who)
-
-    def target(kind, where, who):
-        return part_of((out_d, out_u, out_s), kind, where, who)
-
-    def c_pair(k, kind=2, where=None):
-        return copy_to(0, k, source(kind, where, 1 - core), land0.at[slot_of(k)], partner)
-
-    def c_mine(k, kind=2, where=None):
-        return pltpu.make_async_copy(source(kind, where, core), acc.at[lax.rem(k, FIN_SLOTS)], loc_sem.at[0, slot_of(k)])
+        for number in range(5):
+            @pl.when(mat == number)
+            def _(number=number):
+                fn(number, j)
+
+    def part_of(refs, number, j, who):
+        ref = refs[number]
+        if number == 4:
+            return ref.at[pl.ds(pl.multiple_of(who * SET_ROWS, SET_ROWS), SET_ROWS), :]
+        rows, cols = place(number % 2, j, who)
+        return ref.at[rows, cols]
+
+    sources = (part_d.at[1], part_u.at[1], part_d.at[0], part_u.at[0], part_s)
+    targets = (out_d1, out_u1, None, None, out_s)
+
+    def rows_in_vmem(number, j, who):
+        return pl.ds(pl.multiple_of(((number - 2) * per_mat + j) * 2 * SET_ROWS + who * SET_ROWS, SET_ROWS), SET_ROWS)
+
+    def target(number, j, who):
+        if number in (2, 3):
+            return out_v.at[rows_in_vmem(number, j, who), :]
+        return part_of(targets, number, j, who)
+
+    def c_pair(k, number=4, j=0):
+        return copy_to(0, k, part_of(sources, number, j, 1 - core), land0.at[slot_of(k)], partner)
+
+    def c_mine(k, number=4, j=0):
+        return pltpu.make_async_copy(part_of(sources, number, j, core), acc.at[lax.rem(k, FIN_SLOTS)], loc_sem.at[0, slot_of(k)])
 
     def c_d1(k):
         return copy_to(1, k, rows_of(k, far_half, half), land1.at[slot_of(k)], near1)
@@ -232,19 +234,19 @@
     def c_e1(k):
         return copy_to(9, k, done_of(k, own_half, half), done_of(k, own_half, half), near1)
 
-    def c_out(k, kind=2, where=None):
-        return copy_to(10, k, done_of(k, 0, SET_ROWS), target(kind, where, core), partner)
-
-    def c_loc(k, kind=2, where=None):
-        return pltpu.make_async_copy(done_of(k, 0, SET_ROWS), target(kind, where, core), loc_sem.at[1, slot_of(k)])
+    def c_out(k, number=4, j=0):
+        return copy_to(10, k, done_of(k, 0, SET_ROWS), target(number, j, core), partner)
+
+    def c_loc(k, number=4, j=0):
+        return pltpu.make_async_copy(done_of(k, 0, SET_ROWS), target(number, j, core), loc_sem.at[1, slot_of(k)])
 
     def wait0(k):
         pass
 
     def send0(k):
-        def go(kind, where):
-            c_pair(k, kind, where).start()
-            c_mine(k, kind, where).start()
+        def go(number, j):
+            c_pair(k, number, j).start()
+            c_mine(k, number, j).start()
         by_matrix(k, go)
 
     def wait1(k):
@@ -353,14 +355,21 @@
         c_e1(k).wait()
 
     def send10(k):
-        def go(kind, where):
-            c_out(k, kind, where).start()
-            c_loc(k, kind, where).start()
+        def go(number, j):
+            c_out(k, number, j).start()
+            if number in (2, 3):
+                out_v[rows_in_vmem(number, j, core), :] = fin[lax.rem(k, FIN_SLOTS)]
+            else:
+                c_loc(k, number, j).start()
         by_matrix(k, go)
 
     def wait11(k):
         c_out(k).wait()
-        c_loc(k).wait()
+        mat = k // per_mat
+
+        @pl.when(jnp.logical_not(jnp.logical_or(mat == 2, mat == 3)))
+        def _():
+            c_loc(k).wait()
 
     def send11(k):
         pass
@@ -378,7 +387,7 @@
                 sends[stage](k)
 
 
-    rows = g.shape[0]
+    rows = gb.shape[0]
     blocks = per_mat * 2 * SET_ROWS // width
     half_w = width // 2
     a_steps = 2 * blocks
@@ -400,27 +409,40 @@
     def wait_x(q):
         pltpu.make_async_copy(a_hbm.at[0, :, pl.ds(0, width)], xbuf.at[lax.rem(q, 2)], x_sem.at[lax.rem(q, 2)]).wait()
 
-    def w_copies(p):
-        slot = lax.rem(p, 2)
+    def w_copy(which, p):
         layer = 1 - p // blocks
         span = pl.ds(pl.multiple_of(lax.rem(p, blocks) * width, width), width)
-        return (pltpu.make_async_copy(wd_hbm.at[layer, span, :], wd.at[slot], w_sem.at[0, slot]),
-                pltpu.make_async_copy(wu_hbm.at[layer, :, span], wu.at[slot], w_sem.at[1, slot]))
-
-    def layer_copies(layer):
-        return (pltpu.make_async_copy(n_hbm.at[layer], nbuf, in_sem.at[2]), pltpu.make_async_copy(h_hbm.at[layer], hbuf, in_sem.at[3]))
+        if which == 0:
+            return pltpu.make_async_copy(wd_hbm.at[layer, span, :], wd, w_sem.at[0])
+        return pltpu.make_async_copy(wu_hbm.at[layer, :, span], wu, w_sem.at[1])
+
+    def n_copy(layer):
+        return pltpu.make_async_copy(n_hbm.at[layer], nbuf, in_sem.at[2])
+
+    def h_copy(layer, i):
+        span = pl.ds(pl.multiple_of(i * tile, 16), tile)
+        return pltpu.make_async_copy(h_hbm.at[layer, span, :], htile, in_sem.at[3])
+
+    def g_copy(i):
+        span = pl.ds(pl.multiple_of(i * tile, 16), tile)
+        return pltpu.make_async_copy(g_hbm.at[span, :], gtile, in_sem.at[1])
+
+    def load_rows(layer, i):
+        h_copy(layer, i).start()
+
+        @pl.when(layer == 1)
+        def _():
+            g_copy(i).start()
 
     def result_wait(slot):
         pltpu.make_async_copy(rbuf.at[slot], part_d.at[0, pl.ds(0, half_w), :], r_sem.at[slot]).wait()
 
     load_gb = pltpu.make_async_copy(gb_hbm, gb, in_sem.at[0])
-    load_g = pltpu.make_async_copy(g_hbm, g, in_sem.at[1])
     load_x(jnp.int32(0))
     load_gb.start()
     load_x(jnp.int32(1))
-    for copy in w_copies(jnp.int32(0)):
-        copy.start()
-    load_g.start()
+    w_copy(0, jnp.int32(0)).start()
+    w_copy(1, jnp.int32(0)).start()
     barrier = pltpu.get_barrier_semaphore()
     for peer in (partner, near1, near2, zpair):
         pl.semaphore_signal(barrier, inc=1, device_id=(peer,), device_id_type=MESH)
@@ -441,20 +463,20 @@
 
         @pl.when(w == 0)
         def _():
-            for copy in layer_copies(layer):
-                copy.start()
+            n_copy(layer).start()
             m[...] = jnp.zeros_like(m)
 
         @pl.when(slot == 0)
         def _():
             wait_x(q)
-
-        @pl.when(r >= 2)
-        def _():
-            result_wait(slot)
 
         cols = pl.ds(pl.multiple_of(slot * half_w, 128), half_w)
         rbuf[slot] = lax.dot_general(xbuf[lax.rem(q, 2), :, cols], gb[...], (((0,), (0,)), ((), ())), preferred_element_type=f32)
+
+        @pl.when(r >= 1)
+        def _():
+            result_wait(1 - slot)
+
         out_rows = pl.ds(pl.multiple_of(w * half_w, 128), half_w)
         pltpu.make_async_copy(rbuf.at[slot], part_d.at[layer, out_rows, :], r_sem.at[slot]).start()
 
@@ -469,16 +491,10 @@
         @pl.when(i == 0)
         def _():
             wait_x(q)
-            for copy in w_copies(p):
-                copy.wait()
-
-            @pl.when(p + 1 < 2 * blocks)
-            def _():
-                for copy in w_copies(p + 1):
-                    copy.start()
+            w_copy(0, p).wait()
 
         span = pl.ds(pl.multiple_of(i * tile, 16), tile)
-        e = lax.dot_general(gb[span, :], wd[lax.rem(p, 2)], (((1,), (1,)), ((), ())), preferred_element_type=f32)
+        e = lax.dot_general(gb[span, :], wd[...], (((1,), (1,)), ((), ())), preferred_element_type=f32)
         u = xbuf[lax.rem(q, 2), span, :].astype(f32)
         sq = u * u
         t = jnp.tanh(u * (GELU_C + (GELU_C * GELU_A) * sq))
@@ -493,42 +509,63 @@
         def _():
             load_x(q + 2)
 
+            @pl.when(p + 1 < 2 * blocks)
+            def _():
+                w_copy(0, p + 1).start()
+
     def step_m(layer, block, i):
         p = (1 - layer) * blocks + block
+        @pl.when(i == 0)
+        def _():
+            w_copy(1, p).wait()
+
         span = pl.ds(pl.multiple_of(i * 2 * tile, 16), 2 * tile)
-        m[span, :] = m[span, :] + lax.dot_general(dbuf[span, :], wu[lax.rem(p, 2)], (((1,), (1,)), ((), ())), preferred_element_type=f32)
+        m[span, :] = m[span, :] + lax.dot_general(dbuf[span, :], wu[...], (((1,), (1,)), ((), ())), preferred_element_type=f32)
+
+        @pl.when(jnp.logical_and(i == 1, p + 1 < 2 * blocks))
+        def _():
+            w_copy(1, p + 1).start()
 
     def step_u(layer, block, i):
         @pl.when(jnp.logical_and(block == 0, i == 0))
         def _():
-            for copy in layer_copies(layer):
-                copy.wait()
-
-        result_wait(i)
+            n_copy(layer).wait()
+
         cols = pl.ds(pl.multiple_of(i * half_w, 128), half_w)
         rbuf[i] = lax.dot_general(nbuf[:, cols], dbuf[...], (((0,), (0,)), ((), ())), preferred_element_type=f32)
+        result_wait(1 - i)
         out_cols = pl.ds(pl.multiple_of(block * width, width), width)
         pltpu.make_async_copy(rbuf.at[i], part_u.at[layer, cols, out_cols], r_sem.at[i]).start()
 
+        @pl.when(jnp.logical_and(block == blocks - 1, i == 1))
+        def _():
+            load_rows(layer, 0)
+
     def step_c(layer, i):
-        @pl.when(jnp.logical_and(layer == 1, i == 0))
-        def _():
-            load_g.wait()
-
         span = pl.ds(pl.multiple_of(i * tile, 16), tile)
-        x = hbuf[span, :].astype(f32)
+        h_copy(layer, i).wait()
+        x = htile[...].astype(f32)
         scale = lax.rsqrt(jnp.mean(x * x, axis=-1, keepdims=True) + EPSILON)
         hat = x * scale
         grad_n = m[span, :]
-        old = g[span, :]
         gain_row = pl.ds(layer * small_rows, 1)
-        bias_row = pl.ds(layer * small_rows + blocks + 1, 1)
         sbuf[gain_row, :] = sbuf[gain_row, :] + jnp.sum(grad_n * hat, axis=0, keepdims=True)
-        sbuf[bias_row, :] = sbuf[bias_row, :] + jnp.sum(old, axis=0, keepdims=True)
-        grad_hat = grad_n * row_of(gain, layer)
-        new = old + scale * (grad_hat - hat * jnp.mean(grad_hat * hat, axis=-1, keepdims=True))
-        g[span, :] = new
-        gb[span, :] = new.astype(bf16)
+
+        @pl.when(layer == 1)
+        def _():
+            g_copy(i).wait()
+            old = gtile[...]
+            bias_row = small_rows + blocks + 1
+            sbuf[bias_row : bias_row + 1, :] = sbuf[bias_row : bias_row + 1, :] + jnp.sum(old, axis=0, keepdims=True)
+            grad_hat = grad_n * row_of(gain, layer)
+            new = old + scale * (grad_hat - hat * jnp.mean(grad_hat * hat, axis=-1, keepdims=True))
+            bias_row = blocks + 1
+            sbuf[bias_row : bias_row + 1, :] = sbuf[bias_row : bias_row + 1, :] + jnp.sum(new, axis=0, keepdims=True)
+            gb[span, :] = new.astype(bf16)
+
+        @pl.when(i < 3)
+        def _():
+            load_rows(layer, i + 1)
 
     def compute(s):
         layer = 1 - s // layer_steps
@@ -562,15 +599,14 @@
         @pl.when(s == all_steps)
         def _():
             small_copy.start()
-            result_wait(0)
             result_wait(1)
             small_copy.wait()
 
-        @pl.when(s >= 2)
-        def _():
-            tick(s - 2)
-
-    pl.loop(0, num_sets + STAGES * LAG + 2)(whole_step)
+        @pl.when(s >= 1)
+        def _():
+            tick(s - 1)
+
+    pl.loop(0, num_sets + STAGES * LAG + 1)(whole_step)
 
 
 def backward(axis, g, gb, a, u, n, h, w_down, w_up, norm_gain):
@@ -581,13 +617,16 @@
     piece = SET_ROWS // 8
     any_spec = pl.BlockSpec(memory_space=pl.ANY)
     shape = jax.ShapeDtypeStruct
-    shapes = [shape((2, hidden, width), f32), shape((2, width, hidden), f32), shape((2 * SET_ROWS, width), f32)]
+    small_shape = shape((2 * SET_ROWS, width), f32)
+    shapes = [shape((hidden, width), f32), shape((width, hidden), f32), pltpu.VMEM((2 * hidden, width), f32), small_shape,
+              shape((2, hidden, width), f32), shape((2, width, hidden), f32), small_shape]
+    vmem_spec = pl.BlockSpec(memory_space=pltpu.VMEM)
     return pl.pallas_call(
         functools.partial(backward_kernel, axis, num_sets, per_mat),
         name="backward_and_sum",
-        out_shape=shapes + shapes,
-        in_specs=[any_spec] * 8 + [pl.BlockSpec(memory_space=pltpu.VMEM)],
-        out_specs=[any_spec] * 6,
+        out_shape=shapes,
+        in_specs=[any_spec] * 8 + [vmem_spec],
+        out_specs=[any_spec] * 2 + [vmem_spec] + [any_spec] * 4,
         scratch_shapes=[
             pltpu.VMEM((FIN_SLOTS, SET_ROWS, width), f32),
             pltpu.VMEM((FIN_SLOTS, SET_ROWS, width), f32),
@@ -597,14 +636,14 @@
             pltpu.VMEM((SLOTS, 2 * piece, width), f32),
             pltpu.VMEM((SLOTS, piece, width), f32),
             pltpu.VMEM((SLOTS, piece, width), f32),
-            pltpu.VMEM((rows, width), f32),
             pltpu.VMEM((rows, width), bf16),
             pltpu.VMEM((rows, width), f32),
             pltpu.VMEM((2, rows, width), bf16),
             pltpu.VMEM((rows, width), bf16),
-            pltpu.VMEM((rows, width), bf16),
-            pltpu.VMEM((2, width, width), bf16),
-            pltpu.VMEM((2, width, width), bf16),
+            pltpu.VMEM((rows // 4, width), f32),
+            pltpu.VMEM((rows // 4, width), bf16),
+            pltpu.VMEM((width, width), bf16),
+            pltpu.VMEM((width, width), bf16),
             pltpu.VMEM((rows, width), bf16),
             pltpu.VMEM((2, width // 2, width), f32),
             pltpu.VMEM((2 * SET_ROWS, width), f32),
@@ -612,73 +651,79 @@
             pltpu.SemaphoreType.DMA((STAGES, SLOTS)),
             pltpu.SemaphoreType.DMA((2, SLOTS)),
             pltpu.SemaphoreType.DMA((2,)),
-            pltpu.SemaphoreType.DMA((2, 2)),
+            pltpu.SemaphoreType.DMA((2,)),
             pltpu.SemaphoreType.DMA((2,)),
             pltpu.SemaphoreType.DMA((5,)),
         ],
-        compiler_params=pltpu.CompilerParams(collective_id=0, has_side_effects=True, vmem_limit_bytes=62 * 1024 * 1024),
+        compiler_params=pltpu.CompilerParams(collective_id=0, has_side_effects=True, vmem_limit_bytes=45 * 1024 * 1024),
     )(g, gb, a, u, n, h, w_down, w_up, norm_gain)
 
 
-OUT_RING = 8
-
-
-def emit_kernel(sum_d, sum_u, sum_s, gain_out, up_out, bias_up_out, down_out, bias_down_out, ring_d, ring_u, rows, sem_in, sem_out, sem_s):
-    layers, hidden, width = sum_d.shape
+OUT_RING = 6
+
+
+def emit_kernel(sum_d1, sum_u1, sum_v, sum_s, gain_out, up_out, bias_up_out, down_out, bias_down_out, ring_d, ring_u, rows, sem_in, sem_out, sem_s, sem_v):
+    hidden, width = sum_d1.shape
+    layers = 2
     blocks = hidden // width
     per = blocks + 2
+    down_rows, up_rows = ring_d.shape[1], ring_u.shape[1]
+    parts = hidden // down_rows
+    jobs = []
+    for part in range(parts):
+        for which, (src, ring, dst, step) in enumerate(((sum_d1, ring_d, down_out, down_rows), (sum_u1, ring_u, up_out, up_rows))):
+            span = pl.ds(part * step, step)
+            slot = part % OUT_RING
+            jobs.append((pltpu.make_async_copy(src.at[span, :], ring.at[slot], sem_in.at[which, slot]),
+                         pltpu.make_async_copy(ring.at[slot], dst.at[1, span, :], sem_out.at[which, slot])))
     small = pltpu.make_async_copy(sum_s.at[pl.ds(0, rows.shape[0]), :], rows, sem_s)
-    small.start()
-    down_rows = ring_d.shape[1]
-    up_rows = ring_u.shape[1]
-    jobs = []
-    for layer in range(layers):
-        for part in range(hidden // down_rows):
-            span = pl.ds(part * down_rows, down_rows)
-            jobs.append((sum_d.at[layer, span, :], ring_d, down_out.at[layer, span, :], 0))
-            span = pl.ds(part * up_rows, up_rows)
-            jobs.append((sum_u.at[layer, span, :], ring_u, up_out.at[layer, span, :], 1))
-    reads, writes = [], []
-    for number, (src, ring, dst, which) in enumerate(jobs):
-        slot = (number // 2) % OUT_RING
-        reads.append(pltpu.make_async_copy(src, ring.at[slot], sem_in.at[which, slot]))
-        writes.append(pltpu.make_async_copy(ring.at[slot], dst, sem_out.at[which, slot]))
+    direct = []
+    for block in range(blocks):
+        span = pl.ds(block * width, width)
+        direct.append(pltpu.make_async_copy(sum_v.at[span, :], down_out.at[0, span, :], sem_v.at[0, block]))
+        direct.append(pltpu.make_async_copy(sum_v.at[pl.ds(hidden + block * width, width), :], up_out.at[0, :, span], sem_v.at[1, block]))
     ahead = 2 * OUT_RING
     lead = ahead - 4
+    small.start()
     for number in range(min(lead, len(jobs))):
-        reads[number].start()
+        jobs[number][0].start()
+    for copy in direct:
+        copy.start()
+    small.wait()
+    for layer in range(layers):
+        base = layer * per
+        gain_out[layer : layer + 1, :] = rows[base : base + 1, :]
+        bias_down_out[layer : layer + 1, :] = rows[base + blocks + 1 : base + blocks + 2, :]
+        for block in range(blocks):
+            bias_up_out[layer : layer + 1, block * width : (block + 1) * width] = rows[base + 1 + block : base + 2 + block, :]
     for number in range(len(jobs)):
-        reads[number].wait()
-        writes[number].start()
+        jobs[number][0].wait()
+        jobs[number][1].start()
         follow = number + lead
         if follow < len(jobs):
             if follow >= ahead:
-                writes[follow - ahead].wait()
-            reads[follow].start()
-        if number == 2:
-            small.wait()
-            for layer in range(layers):
-                base = layer * per
-                gain_out[layer : layer + 1, :] = rows[base : base + 1, :]
-                bias_down_out[layer : layer + 1, :] = rows[base + blocks + 1 : base + blocks + 2, :]
-                for block in range(blocks):
-                    bias_up_out[layer : layer + 1, block * width : (block + 1) * width] = rows[base + 1 + block : base + 2 + block, :]
+                jobs[follow - ahead][1].wait()
+            jobs[follow][0].start()
     for number in range(max(0, len(jobs) - ahead), len(jobs)):
-        writes[number].wait()
-
-
-def emit(sum_d, sum_u, sum_s):
-    layers, hidden, width = sum_d.shape
+        jobs[number][1].wait()
+    for copy in direct:
+        copy.wait()
+
+
+def emit(sum_d1, sum_u1, sum_v, sum_s):
+    hidden, width = sum_d1.shape
+    layers = 2
     blocks = hidden // width
     any_spec = pl.BlockSpec(memory_space=pl.ANY)
     vmem_spec = pl.BlockSpec(memory_space=pltpu.VMEM)
+    hbm_spec = pl.BlockSpec(memory_space=pltpu.HBM)
     shape = jax.ShapeDtypeStruct
     return pl.pallas_call(
         emit_kernel,
         name="emit",
         out_shape=[shape((layers, width), f32), shape((layers, width, hidden), f32), shape((layers, hidden), f32),
                    shape((layers, hidden, width), f32), shape((layers, width), f32)],
-        in_specs=[any_spec] * 3,
+        in_specs=[hbm_spec] * 2 + [vmem_spec] + [hbm_spec],
         out_specs=[vmem_spec, any_spec, vmem_spec, any_spec, vmem_spec],
         scratch_shapes=[
             pltpu.VMEM((OUT_RING, hidden // 8, width), f32),
@@ -687,9 +732,10 @@
             pltpu.SemaphoreType.DMA((2, OUT_RING)),
             pltpu.SemaphoreType.DMA((2, OUT_RING)),
             pltpu.SemaphoreType.DMA,
+            pltpu.SemaphoreType.DMA((2, blocks)),
         ],
-        compiler_params=pltpu.CompilerParams(vmem_limit_bytes=60 * 1024 * 1024),
-    )(sum_d, sum_u, sum_s)
+        compiler_params=pltpu.CompilerParams(vmem_limit_bytes=40 * 1024 * 1024),
+    )(sum_d1, sum_u1, pltpu.with_memory_space_constraint(sum_v, pltpu.VMEM), sum_s)
 
 
 def solution(mesh):
@@ -697,8 +743,8 @@
 
     def device_grads(tokens, upstream, norm_gain, w_up, bias_up, w_down, bias_down):
         u, a, h, n, g, gb = forward(tokens, upstream, norm_gain, w_up, bias_up, w_down, bias_down)
-        out_d, out_u, out_s = backward(data_axis, g, gb, a, u, n, h, w_down, w_up, norm_gain)[:3]
-        return tuple(emit(out_d, out_u, out_s))
+        sums = backward(data_axis, g, gb, a, u, n, h, w_down, w_up, norm_gain)[:4]
+        return tuple(emit(*sums))
 
     row_spec = P(data_axis, None)
     full_spec = P()

time: 360 us -> 352 us (0.978)
  Pallas kernels: 359 us -> 351 us
    pallas_call x1, Pallas kernels: 25.6 us -> 20.2 us  [emit(): pl.pallas_call(emit_kernel, name='emit', out_shape=[shape((layers, width)...]
where the time goes in v4:
time: 352 us
  Pallas kernels  351 us (100%)
    pallas_call x1, Pallas kernels, backward(): pl.pallas_call(functools.partial(backward_kernel, axis, num_sets, per_mat...  269 us
    pallas_call x1, Pallas kernels, forward(): pl.pallas_call(forward_kernel, name='forward', grid=grid, in_specs=[pl.Bl...  61.7 us
    pallas_call x1, Pallas kernels, emit(): pl.pallas_call(emit_kernel, name='emit', out_shape=[shape((layers, width)...  20.2 us

profile of v4, /device:TPU:0, one launch (start us, length us, event | category | flops | bytes accessed | tf_op | source)
XLA Modules:
  0.0 351.8 jit_solution(14517229661413809851)
XLA Ops:
  0.6 61.7 %forward.1 = (bf16[2,2048,3072]{2,1,0:T(8,128)(2,1)}, bf16[2,2048,3072]{2,1,0:T(8,128)(2,1)}, bf16[2,2048,768]{2,1,0:T(8,128)(2,1)}, bf16[2,2048,768]{2,1,0:T(8,...) custom-call(bf16[2048,768]{1,0:T(8,128)(2,1)} %tok.1, bf16[2048,768]{1,0:T(8,128)(2,1)} %up.1, ...), custom_call_target="tpu_custom_call" | custom-call | tf_op jit(solution)/shard_map/forward/pallas_call | solution.py:83
  62.3 269.1 %backward_and_sum.1 = (f32[3072,768]{1,0:T(8,128)}, f32[768,3072]{1,0:T(8,128)}, f32[6144,768]{1,0:T(8,128)S(1)}, f32[128,768]{1,0:T(8,128)}, f32[2,3072,768]{2,...) custom-call(f32[2048,768]{1,0:T(8,128)} %get-tuple-element.15.g_hbm, ...), custom_call_target="tpu_custom_call" | custom-call | tf_op jit(solution)/shard_map/backward_and_sum/pallas_call | solution.py:624
  331.5 20.2 %emit.1 = (f32[2,768]{1,0:T(2,128)}, f32[2,768,3072]{2,1,0:T(8,128)}, f32[2,3072]{1,0:T(2,128)}, f32[2,3072,768]{2,1,0:T(8,128)}, f32[2,768]{1,0:T(2,128)}) custom-call(f32[3072,768]{1,0:T(8,128)} %get-tuple-element.21.sum_d1, f32[768,3072]{1,0:T(8,128)} %get-tuple-element.22.sum_u1, f32[6144,768]{1,0:T(8,128)S(1)} %get-tuple-element.23.sum_v, ...), custom_call_target="tpu_custom_call" | custom-call | tf_op jit(solution)/shard_map/emit/pallas_call | solution.py:721
